TPU v7x, 32 devices: a whole 2x2x4 slice. The times are simulated.
32 devices in a mesh: rows: 8 (over z, x), cols: 4 (over y, core).
Axes of the slice: x: 2, y: 2, z: 4, core: 2. Of those that a mesh axis runs over, the one named last changes fastest.
Arguments:
- panel: float32 [4096, 1024], P('rows'), as said below
- window_block: float32 [4096, 2048], P('rows', 'cols'), may hold values from -6 to 6
- row_live: int32 [8], replicated, may hold values 0 or 1
- window_rows: int32 [4], replicated, may hold values from 2 to 7, as said below
Outputs:
- factor: float32 [4096, 1024], P('rows')
- updated: float32 [4096, 2048], P('rows', 'cols')
Inputs may be any that keep to these rules, and one draw needn't show every extreme that they name: `window_rows`: distinct tile rows, none inside the supernode. `row_live`: the value for tile rows below 2 is ignored: those rows are always present. `panel`: the first 1024 rows hold a symmetric positive definite block.
All inputs are finite; a program needn't handle non-finite values.
Results may differ from a plain program's by a relative error of at most 0.0001.
Values sent between devices are 32-bit elements; how exact they have to be, the bound alone decides.
A program may use at most 128 MiB of HBM per device.

v0:
```python
import functools

import jax
import jax.numpy as jnp
from jax import lax
from jax.experimental import pallas as pl
from jax.experimental.pallas import tpu as pltpu
from jax.sharding import PartitionSpec as P

P_SIZE = 2
HIGHEST = lax.Precision.HIGHEST
CONTRACT = (((1,), (1,)), ((), ()))
PLAIN = (((1,), (0,)), ((), ()))
LEAF = 128
GROUP = 16
WIDE = 256
MESH = pl.DeviceIdType.MESH


def halves(value):
    high = value.astype(jnp.bfloat16)
    return high, (value - high.astype(jnp.float32)).astype(jnp.bfloat16)


def product(left, right, contract):
    lh, ll = halves(left)
    rh, rl = halves(right)

    def dot(a, b):
        return lax.dot_general(a, b, contract, preferred_element_type=jnp.float32)

    return dot(lh, rh) + (dot(lh, rl) + dot(ll, rh))


def times_trans(left, right):
    return product(left, right, CONTRACT)


def times(left, right):
    return product(left, right, PLAIN)


def spread_kernel(n_rows, panel, first, second, row_send, row_recv, far_send, far_recv, near_send, near_recv):
    r = lax.axis_index("rows")
    c = lax.axis_index("cols")
    far = lax.rem(c + 2, 4)
    near = c + 1 - 2 * lax.rem(c, 2)
    width = panel.shape[0]
    n_blocks = width // LEAF
    share = LEAF // 4
    pieces = [(which, b) for which in range(2) for b in range(n_blocks)]

    barrier = pltpu.get_barrier_semaphore()
    for other in (far, near):
        pl.semaphore_signal(barrier, inc=1, device_id=(r, other), device_id_type=MESH)

    @pl.when(r < 2)
    def _():
        pl.semaphore_signal(barrier, inc=1, device_id=(1 - r, c), device_id_type=MESH)

    @pl.when(r >= 2)
    def _():
        pl.semaphore_signal(barrier, inc=1, device_id=(r - 2, c), device_id_type=MESH)

    @pl.when(r + 2 < n_rows)
    def _():
        pl.semaphore_signal(barrier, inc=1, device_id=(r + 2, c), device_id_type=MESH)

    pl.semaphore_wait(barrier, 3 + (r + 2 < n_rows).astype(jnp.int32))

    def window(ref, piece, owner):
        which, b = pieces[piece]
        start = pl.multiple_of(b * LEAF + owner * share, 8)
        return ref.at[pl.ds(start, share), pl.ds(0, which * width + (b + 1) * LEAF)]

    def landing(piece, owner):
        return window((first, second)[pieces[piece][0]], piece, owner)

    def to_row(piece, slot, dest, own):
        return pltpu.make_async_remote_copy(
            src_ref=window(panel, piece, c) if own else landing(piece, c), dst_ref=landing(piece, c),
            send_sem=row_send.at[piece, slot], recv_sem=row_recv.at[piece],
            device_id=(dest, c), device_id_type=MESH)

    def to_far(piece):
        return pltpu.make_async_remote_copy(
            src_ref=landing(piece, c), dst_ref=landing(piece, c),
            send_sem=far_send.at[piece], recv_sem=far_recv.at[piece],
            device_id=(r, far), device_id_type=MESH)

    def to_near(piece, slot):
        owner = (c, far)[slot]
        return pltpu.make_async_remote_copy(
            src_ref=landing(piece, owner), dst_ref=landing(piece, owner),
            send_sem=near_send.at[piece, slot], recv_sem=near_recv.at[piece, slot],
            device_id=(r, near), device_id_type=MESH)

    for piece in range(len(pieces)):
        which = pieces[piece][0]

        @pl.when(r == which)
        def _():
            to_row(piece, 0, 1 - which, True).start()
            if which + 2 < n_rows:
                to_row(piece, 1, which + 2, True).start()

    @pl.when(r == 0)
    def _():
        first[...] = panel[:, :width]

    @pl.when(r == 1)
    def _():
        second[...] = panel[...]

    for piece in range(len(pieces) + 1):
        if piece < len(pieces):

            @pl.when(r != pieces[piece][0])
            def _():
                to_row(piece, 0, r, False).wait_recv()

                @pl.when(r + 2 < n_rows)
                def _():
                    to_row(piece, 0, r + 2, False).start()

                to_far(piece).start()
                to_near(piece, 0).start()

        if piece > 0:

            @pl.when(r != pieces[piece - 1][0])
            def _():
                to_far(piece - 1).wait_recv()
                to_near(piece - 1, 1).start()

    for piece in range(len(pieces)):
        which = pieces[piece][0]

        @pl.when(r != which)
        def _():
            for slot in range(2):
                to_near(piece, slot).wait_recv()
            for slot in range(2):
                to_near(piece, slot).wait_send()
            to_far(piece).wait_send()

            @pl.when(r + 2 < n_rows)
            def _():
                to_row(piece, 0, r + 2, False).wait_send()

        @pl.when(r == which)
        def _():
            to_row(piece, 0, 1 - which, True).wait_send()
            if which + 2 < n_rows:
                to_row(piece, 1, which + 2, True).wait_send()


def spread(panel, n_rows, n_cols):
    if n_cols != 4 or n_rows < 2:
        raise ValueError("unsupported mesh")
    width = panel.shape[0]
    n_pieces = 2 * (width // LEAF)
    return pl.pallas_call(
        functools.partial(spread_kernel, n_rows),
        out_shape=(
            jax.ShapeDtypeStruct((width, width), jnp.float32),
            jax.ShapeDtypeStruct((width, P_SIZE * width), jnp.float32),
        ),
        in_specs=[pl.BlockSpec(memory_space=pltpu.VMEM)],
        out_specs=(pl.BlockSpec(memory_space=pltpu.VMEM),) * 2,
        scratch_shapes=[
            pltpu.SemaphoreType.DMA((n_pieces, 2)),
            pltpu.SemaphoreType.DMA((n_pieces,)),
            pltpu.SemaphoreType.DMA((n_pieces,)),
            pltpu.SemaphoreType.DMA((n_pieces,)),
            pltpu.SemaphoreType.DMA((n_pieces, 2)),
            pltpu.SemaphoreType.DMA((n_pieces, 2)),
        ],
        compiler_params=pltpu.CompilerParams(
            collective_id=0, has_side_effects=True, vmem_limit_bytes=24 << 20),
        cost_estimate=pl.CostEstimate(flops=10**9, bytes_accessed=10**7, transcendentals=0),
        name="spread",
    )(panel)


def split3(value):
    high = value.astype(jnp.bfloat16).astype(jnp.float32)
    rest = value - high
    mid = rest.astype(jnp.bfloat16).astype(jnp.float32)
    return high, mid, rest - mid


def factor_leaf(aug, upper, inverse):
    lanes = lax.broadcasted_iota(jnp.int32, (GROUP, LEAF), 1)
    subs = lax.broadcasted_iota(jnp.int32, (GROUP, LEAF), 0)
    for g in range(LEAF // GROUP):
        base = g * GROUP
        left = aug[base : base + GROUP, :LEAF]
        right = aug[base : base + GROUP, LEAF:]
        cols = [
            jnp.broadcast_to(left[:, base + j : base + j + 1], (GROUP, LEAF)) for j in range(GROUP)
        ]
        scale = jnp.zeros((GROUP, LEAF), jnp.float32)
        for k in range(GROUP):
            pivot = jnp.broadcast_to(cols[k][k : k + 1, :], (GROUP, LEAF))
            root = lax.rsqrt(pivot)
            scale = jnp.where(subs == k, root, scale)
            if k + 1 < GROUP:
                mult = jnp.where(subs > k, cols[k] * (root * root), 0.0)
                for j in range(k + 1, GROUP):
                    cols[j] = cols[j] - mult * jnp.broadcast_to(cols[j][k : k + 1, :], (GROUP, LEAF))
                left = left - mult * jnp.broadcast_to(left[k : k + 1, :], (GROUP, LEAF))
                right = right - mult * jnp.broadcast_to(right[k : k + 1, :], (GROUP, LEAF))
        row_of = lanes - base
        left = jnp.where(row_of >= subs, left * scale, 0.0)
        right = right * scale
        upper[base : base + GROUP, :] = left
        inverse[base : base + GROUP, :] = right
        if base + GROUP < LEAF:
            lh, lm, ll = split3(left)
            rh, rm, rl = split3(right)
            keep = lanes >= base + GROUP
            a = [jnp.where(keep, v, 0.0) for v in (lh, lm, ll)]
            lhs = jnp.concatenate([a[0], a[0], a[1], a[0], a[1], a[2]], axis=0)
            rl_ = jnp.concatenate([lh, lm, lh, ll, lm, lh], axis=0)
            rr_ = jnp.concatenate([rh, rm, rh, rl, rm, rh], axis=0)
            rhs = jnp.concatenate([rl_, rr_], axis=1)
            update = lax.dot_general(
                lhs, rhs, (((0,), (0,)), ((), ())), preferred_element_type=jnp.float32)
            aug[base + GROUP :, :] = aug[base + GROUP :, :] - update[base + GROUP :, :]


def factor_kernel(live, first, second, panel, factor, solved, lower, inverses, aug, upper, leaf_inv):
    width = first.shape[0]
    total = lower.shape[0]
    n_leaf = total // LEAF
    per = width // LEAF
    rows = lax.broadcasted_iota(jnp.int32, (LEAF, LEAF), 0)
    lanes = lax.broadcasted_iota(jnp.int32, (LEAF, LEAF), 1)
    lower[:width, :width] = first[...]
    lower[:width, width:] = jnp.zeros((width, total - width), jnp.float32)
    lower[width:, :] = second[...]
    for b in range(n_leaf - 1):
        lower[b * LEAF : (b + 1) * LEAF, (b + 1) * LEAF :] = jnp.zeros(
            (LEAF, total - (b + 1) * LEAF), jnp.float32)
    inverses[...] = jnp.zeros(inverses.shape, jnp.float32)

    def step(k, carry):
        at = pl.ds(pl.multiple_of(k * LEAF, LEAF), LEAF)
        block = lower[at, at]
        aug[:, :LEAF] = jnp.where(rows >= lanes, block, block.T)
        aug[:, LEAF:] = jnp.where(rows == lanes, 1.0, 0.0)
        factor_leaf(aug, upper, leaf_inv)
        lower[at, at] = upper[...].T
        for b in range(n_leaf):

            @pl.when(k == b)
            def _():
                lo, hi = b * LEAF, (b + 1) * LEAF
                wide = b * LEAF // WIDE
                off = lo - wide * WIDE
                inv = leaf_inv[...]
                inverses[wide, off : off + LEAF, off : off + LEAF] = inv
                if off:
                    before = inverses[wide, :LEAF, :LEAF]
                    cross = lower[lo:hi, lo - LEAF : lo]
                    part = lax.dot_general(
                        cross, before, (((1,), (0,)), ((), ())), precision=HIGHEST,
                        preferred_element_type=jnp.float32)
                    inverses[wide, LEAF:, :LEAF] = -lax.dot_general(
                        inv, part, (((1,), (0,)), ((), ())), precision=HIGHEST,
                        preferred_element_type=jnp.float32)
                if hi < total:
                    lower[hi:, lo:hi] = times_trans(lower[hi:, lo:hi], inv)
                    nxt = hi + LEAF
                    lower[hi:, hi:nxt] = lower[hi:, hi:nxt] - times_trans(
                        lower[hi:, :hi], lower[hi:nxt, :hi])

        return carry

    lax.fori_loop(0, n_leaf, step, 0)

    r = lax.axis_index("rows")
    n_wide = total // WIDE

    @pl.when(r < P_SIZE)
    def _():
        factor[...] = lower[pl.ds(pl.multiple_of(lax.rem(r, P_SIZE) * width, width), width), :]

    @pl.when(r >= P_SIZE)
    def _():
        factor[...] = panel[...] * live[0]
        for wide in range(n_wide):
            lo, hi = wide * WIDE, (wide + 1) * WIDE
            now = factor[:, lo:hi]
            if wide:
                now = now - times_trans(factor[:, :lo], lower[lo:hi, :lo])
            factor[:, lo:hi] = times_trans(now, inverses[wide])

    for wide in reversed(range(n_wide)):
        lo, hi = wide * WIDE, (wide + 1) * WIDE
        now = factor[:, lo:hi]
        if hi < total:
            now = now - times(solved[:, hi:], lower[hi:, lo:hi])
        solved[:, lo:hi] = times(now, inverses[wide])


def factor_rows(live, first, second, panel):
    width = first.shape[0]
    total = P_SIZE * width
    return pl.pallas_call(
        factor_kernel,
        out_shape=(jax.ShapeDtypeStruct(panel.shape, jnp.float32),) * 2,
        in_specs=[pl.BlockSpec(memory_space=pltpu.SMEM)] + [pl.BlockSpec(memory_space=pltpu.VMEM)] * 3,
        out_specs=(pl.BlockSpec(memory_space=pltpu.VMEM),) * 2,
        scratch_shapes=[
            pltpu.VMEM((total, total), jnp.float32),
            pltpu.VMEM((total // WIDE, WIDE, WIDE), jnp.float32),
            pltpu.VMEM((LEAF, 2 * LEAF), jnp.float32),
            pltpu.VMEM((LEAF, LEAF), jnp.float32),
            pltpu.VMEM((LEAF, LEAF), jnp.float32),
        ],
        compiler_params=pltpu.CompilerParams(vmem_limit_bytes=40 << 20),
        cost_estimate=pl.CostEstimate(flops=10**10, bytes_accessed=10**7, transcendentals=0),
        name="factor_rows",
    )(live, first, second, panel)


def update_kernel(solved, target, window, updated):
    updated[...] = window[...] - times_trans(solved[...], target[...])


def update_window(solved, target, window):
    return pl.pallas_call(
        update_kernel,
        out_shape=jax.ShapeDtypeStruct(window.shape, jnp.float32),
        in_specs=[pl.BlockSpec(memory_space=pltpu.VMEM)] * 3,
        out_specs=pl.BlockSpec(memory_space=pltpu.VMEM),
        compiler_params=pltpu.CompilerParams(vmem_limit_bytes=40 << 20),
        cost_estimate=pl.CostEstimate(flops=10**9, bytes_accessed=10**7, transcendentals=0),
        name="update_window",
    )(solved, target, window)


def shards(n_rows, n_cols, panel, window_block, row_live, window_rows):
    device_row = lax.axis_index("rows")
    device_col = lax.axis_index("cols")
    live = jnp.where(device_row < P_SIZE, 1, row_live[device_row]).astype(jnp.float32)
    target = window_rows[device_col]
    kept = jnp.where(device_row == target, panel * live, 0)
    kept, panel = lax.optimization_barrier((kept, panel))
    target_raw = lax.psum(kept, "rows")
    first, second = spread(panel, n_rows, n_cols)
    factor, solved = factor_rows(live[None], first, second, panel)
    updated = update_window(solved, target_raw, window_block)
    return (factor, updated)


def solution(mesh):
    in_specs = (P("rows", None), P("rows", "cols"), P(), P())
    out_specs = (P("rows", None), P("rows", "cols"))
    body = functools.partial(shards, mesh.shape["rows"], mesh.shape["cols"])
    return jax.shard_map(body, mesh=mesh, in_specs=in_specs, out_specs=out_specs, check_vma=False)
```

profile of v0, /device:TPU:0, one launch (start us, length us, event | category | flops | bytes accessed | tf_op | source)
XLA Modules:
  0.0 141.4 jit_solution(3059885506120330226)
XLA Ops:
  7.2 0.0 all-reduce.2.cloned.1.call-start
  7.2 1.2 dynamic_slice.7
  9.1 1.2 dynamic_slice.6
  11.0 3.3 %multiply_select_fusion = f32[512,1024]{1,0:T(8,128)} fusion(f32[512,1024]{1,0:T(8,128)} %panel.1, f32[]{:T(128)} %convert_element_type.5, pred[]{:T(512)S(6)} %eq.3), kind=kLoop, calls=%fused_computation | loop fusion | flops 1048576 | bytes 4194309 | tf_op jit(solution)/shard_map/jit(_where)/select_n | solution.py:350
  14.3 0.0 copy-start.1
  14.3 0.0 all-reduce.2.cloned.1.call-update
  14.3 1.6 %copy-done.1 = f32[512,1024]{1,0:T(8,128)S(1)} copy-done((f32[512,1024]{1,0:T(8,128)S(1)}, f32[512,1024]{1,0:T(8,128)}, u32[]{:S(2)}) %copy-start.1) | copy-done | bytes 2097176
  15.9 0.0 copy-start.2
  15.9 27.2 %spread.1 = (f32[512,512]{1,0:T(8,128)S(1)}, f32[512,1024]{1,0:T(8,128)S(1)}) custom-call(f32[512,1024]{1,0:T(8,128)S(1)} %copy-done.1), custom_call_target="tpu_custom_call" | custom-call | flops 1000000000 | bytes 10000000 | tf_op jit(solution)/shard_map/spread/pallas_call | solution.py:163
  43.1 0.0 copy-done.2
  43.1 0.0 copy-start.3
  43.1 43.5 %factor_rows.1 = (f32[512,1024]{1,0:T(8,128)}, f32[512,1024]{1,0:T(8,128)S(1)}) custom-call(f32[1]{0:T(128)} %bitcast.1.live, f32[512,512]{1,0:T(8,128)S(1)} %get-tuple-element.9.first, f32[512,1024]{1,0:T(8,128)S(1)} %get-tuple-element.10.second, f32[512,1024]{1,0:T(8,128)S(1)} %copy-done.2), custom_call_target="tpu_custom_call" | custom-call | flops 10000000000 | bytes 10000000 | tf_op jit(solution)/shard_map/factor_rows/pallas_call | solution.py:311
  86.6 43.5 %all-reduce.2.cloned.1.call-done.target = f32[512,1024]{1,0:T(8,128)} async-done(((f32[512,1024]{1,0:T(8,128)}), f32[512,1024]{1,0:T(8,128)}) %all-reduce.2.cloned.1.call-update) | async-done | bytes 2097168 | tf_op jit(solution)/shard_map/psum | solution.py:352
  130.1 0.0 copy-done.3
  130.2 0.0 copy-start
  130.2 1.6 %copy-done = f32[512,1024]{1,0:T(8,128)S(1)} copy-done((f32[512,1024]{1,0:T(8,128)S(1)}, f32[512,1024]{1,0:T(8,128)}, u32[]{:S(2)}) %copy-start) | copy-done | bytes 2097176
  131.7 2.8 %update_window.1 = f32[512,512]{1,0:T(8,128)} custom-call(f32[512,1024]{1,0:T(8,128)S(1)} %get-tuple-element.12.solved, f32[512,1024]{1,0:T(8,128)S(1)} %copy-done, f32[512,512]{1,0:T(8,128)S(1)} %copy-done.3), custom_call_target="tpu_custom_call" | custom-call | flops 1000000000 | bytes 10000000 | tf_op jit(solution)/shard_map/update_window/pallas_call | solution.py:334
Async XLA Ops:
  7.2 123.0 %all-reduce.2.cloned.1.call-start = ((), (), s32[]{:S(2)}) async-start(), calls=%async_computation | async-start | bytes 4194304 | tf_op jit(solution)/shard_map/psum | solution.py:352
  14.3 1.6 %copy-start.1 = (f32[512,1024]{1,0:T(8,128)S(1)}, f32[512,1024]{1,0:T(8,128)}, u32[]{:S(2)}) copy-start(f32[512,1024]{1,0:T(8,128)} %panel.1) | copy-start | bytes 6291460
  15.9 27.2 %copy-start.2 = (f32[512,1024]{1,0:T(8,128)S(1)}, f32[512,1024]{1,0:T(8,128)}, u32[]{:S(2)}) copy-start(f32[512,1024]{1,0:T(8,128)} %panel.1) | copy-start | bytes 6291460
  43.1 87.1 %copy-start.3 = (f32[512,512]{1,0:T(8,128)S(1)}, f32[512,512]{1,0:T(8,128)}, u32[]{:S(2)}) copy-start(f32[512,512]{1,0:T(8,128)} %window.1) | copy-start | bytes 3145732
  130.2 1.6 %copy-start = (f32[512,1024]{1,0:T(8,128)S(1)}, f32[512,1024]{1,0:T(8,128)}, u32[]{:S(2)}) copy-start(f32[512,1024]{1,0:T(8,128)} %all-reduce.2.cloned.1.call-done.target) | copy-start | bytes 6291460
Sparse Core Ops, SparseCore 0:
  14.4 115.6 all-reduce.1
where the time goes:
time: 142 us; the launch traced here: 141 us
  Pallas kernels  73.5 us (52%)
  waiting for transfers between devices  43.5 us (31%)
  between operations  15.4 us (11%)
  local copies, waits for them, and re-layouts  5.65 us (4%)
  other arithmetic  3.29 us (2%)
    pallas_call x1, Pallas kernels, factor_rows(): pl.pallas_call(factor_kernel, out_shape=(jax.ShapeDtypeStruct(panel.shape...  43.5 us
    psum x1, waiting for transfers between devices, shards(): target_raw = lax.psum(kept, 'rows')  43.5 us
    pallas_call x1, Pallas kernels, spread(): pl.pallas_call(functools.partial(spread_kernel, n_rows), out_shape=(jax.S...  27.2 us
    select_n x1, other arithmetic, shards(): kept = jnp.where(device_row == target, panel * live, 0)  3.29 us
    unnamed x8, local copies, waits for them, and re-layouts  3.17 us
  transfers between devices with their start and end apart: 1, of which 1 were waited for; matrix products, arithmetic and copies ran while one was open for 0% of the time, Pallas kernels for 50%

commit v1 on v0

--- a/solution.py
+++ b/solution.py
@@ -153,34 +153,6 @@
             to_row(piece, 0, 1 - which, True).wait_send()
             if which + 2 < n_rows:
                 to_row(piece, 1, which + 2, True).wait_send()
-
-
-def spread(panel, n_rows, n_cols):
-    if n_cols != 4 or n_rows < 2:
-        raise ValueError("unsupported mesh")
-    width = panel.shape[0]
-    n_pieces = 2 * (width // LEAF)
-    return pl.pallas_call(
-        functools.partial(spread_kernel, n_rows),
-        out_shape=(
-            jax.ShapeDtypeStruct((width, width), jnp.float32),
-            jax.ShapeDtypeStruct((width, P_SIZE * width), jnp.float32),
-        ),
-        in_specs=[pl.BlockSpec(memory_space=pltpu.VMEM)],
-        out_specs=(pl.BlockSpec(memory_space=pltpu.VMEM),) * 2,
-        scratch_shapes=[
-            pltpu.SemaphoreType.DMA((n_pieces, 2)),
-            pltpu.SemaphoreType.DMA((n_pieces,)),
-            pltpu.SemaphoreType.DMA((n_pieces,)),
-            pltpu.SemaphoreType.DMA((n_pieces,)),
-            pltpu.SemaphoreType.DMA((n_pieces, 2)),
-            pltpu.SemaphoreType.DMA((n_pieces, 2)),
-        ],
-        compiler_params=pltpu.CompilerParams(
-            collective_id=0, has_side_effects=True, vmem_limit_bytes=24 << 20),
-        cost_estimate=pl.CostEstimate(flops=10**9, bytes_accessed=10**7, transcendentals=0),
-        name="spread",
-    )(panel)
 
 
 def split3(value):
@@ -305,25 +277,39 @@
         solved[:, lo:hi] = times(now, inverses[wide])
 
 
-def factor_rows(live, first, second, panel):
-    width = first.shape[0]
+def fused_kernel(n_rows, live, panel, factor, solved, first, second, lower, inverses, aug, upper, leaf_inv, *sems):
+    spread_kernel(n_rows, panel, first, second, *sems)
+    factor_kernel(live, first, second, panel, factor, solved, lower, inverses, aug, upper, leaf_inv)
+
+
+def factor_rows(live, panel, n_rows, n_cols):
+    width = panel.shape[0]
+    n_pieces = 2 * (width // LEAF)
     total = P_SIZE * width
     return pl.pallas_call(
-        factor_kernel,
+        functools.partial(fused_kernel, n_rows),
         out_shape=(jax.ShapeDtypeStruct(panel.shape, jnp.float32),) * 2,
-        in_specs=[pl.BlockSpec(memory_space=pltpu.SMEM)] + [pl.BlockSpec(memory_space=pltpu.VMEM)] * 3,
+        in_specs=[pl.BlockSpec(memory_space=pltpu.SMEM)] + [pl.BlockSpec(memory_space=pltpu.VMEM)],
         out_specs=(pl.BlockSpec(memory_space=pltpu.VMEM),) * 2,
         scratch_shapes=[
+            pltpu.VMEM((width, width), jnp.float32),
+            pltpu.VMEM((width, total), jnp.float32),
             pltpu.VMEM((total, total), jnp.float32),
             pltpu.VMEM((total // WIDE, WIDE, WIDE), jnp.float32),
             pltpu.VMEM((LEAF, 2 * LEAF), jnp.float32),
             pltpu.VMEM((LEAF, LEAF), jnp.float32),
             pltpu.VMEM((LEAF, LEAF), jnp.float32),
+            pltpu.SemaphoreType.DMA((n_pieces, 2)),
+            pltpu.SemaphoreType.DMA((n_pieces,)),
+            pltpu.SemaphoreType.DMA((n_pieces,)),
+            pltpu.SemaphoreType.DMA((n_pieces,)),
+            pltpu.SemaphoreType.DMA((n_pieces, 2)),
+            pltpu.SemaphoreType.DMA((n_pieces, 2)),
         ],
-        compiler_params=pltpu.CompilerParams(vmem_limit_bytes=40 << 20),
+        compiler_params=pltpu.CompilerParams(collective_id=0, has_side_effects=True, vmem_limit_bytes=40 << 20),
         cost_estimate=pl.CostEstimate(flops=10**10, bytes_accessed=10**7, transcendentals=0),
         name="factor_rows",
-    )(live, first, second, panel)
+    )(live, panel)
 
 
 def update_kernel(solved, target, window, updated):
@@ -350,8 +336,7 @@
     kept = jnp.where(device_row == target, panel * live, 0)
     kept, panel = lax.optimization_barrier((kept, panel))
     target_raw = lax.psum(kept, "rows")
-    first, second = spread(panel, n_rows, n_cols)
-    factor, solved = factor_rows(live[None], first, second, panel)
+    factor, solved = factor_rows(live[None], panel, n_rows, n_cols)
     updated = update_window(solved, target_raw, window_block)
     return (factor, updated)
 

time: 142 us -> 143 us (level)
  local copies, waits for them, and re-layouts: 5.65 us -> 8.3 us
    unnamed x8 -> x11, local copies, waits for them, and re-layouts: 3.17 us -> 5.82 us
    pallas_call x2 -> x1, Pallas kernels: 70.7 us -> 70.7 us  [factor_rows(): pl.pallas_call(functools.partial(fused_kernel, n_rows), out_shape=(jax.Sh...]
where the time goes in v1:
time: 143 us
  Pallas kernels  73.5 us (51%)
  waiting for transfers between devices  42.2 us (30%)
  between operations  15.4 us (11%)
  local copies, waits for them, and re-layouts  8.3 us (6%)
  other arithmetic  3.29 us (2%)
    pallas_call x1, Pallas kernels, factor_rows(): pl.pallas_call(functools.partial(fused_kernel, n_rows), out_shape=(jax.Sh...  70.7 us
    psum x1, waiting for transfers between devices, shards(): target_raw = lax.psum(kept, 'rows')  42.2 us
    unnamed x11, local copies, waits for them, and re-layouts  5.82 us
    select_n x1, other arithmetic, shards(): kept = jnp.where(device_row == target, panel * live, 0)  3.29 us
  transfers between devices with their start and end apart: 1, of which 1 were waited for; matrix products, arithmetic and copies ran while one was open for 0% of the time, Pallas kernels for 50%

profile of v1, /device:TPU:0, one launch (start us, length us, event | category | flops | bytes accessed | tf_op | source)
XLA Modules:
  0.0 142.7 jit_solution(10534338456433067273)
XLA Ops:
  7.2 0.0 all-reduce.2.cloned.1.call-start
  7.2 1.2 dynamic_slice.7
  9.1 1.2 dynamic_slice.6
  11.0 3.3 %multiply_select_fusion = f32[512,1024]{1,0:T(8,128)} fusion(f32[512,1024]{1,0:T(8,128)} %panel, f32[]{:T(128)} %convert_element_type.5, pred[]{:T(512)S(6)} %eq.3), kind=kLoop, calls=%fused_computation | loop fusion | flops 1048576 | bytes 4194309 | tf_op jit(solution)/shard_map/jit(_where)/select_n | solution.py:336
  14.3 0.0 all-reduce.2.cloned.1.call-update
  14.3 0.0 copy-start.1
  14.3 1.6 %copy-done.1 = f32[512,1024]{1,0:T(8,128)S(1)} copy-done((f32[512,1024]{1,0:T(8,128)S(1)}, f32[512,1024]{1,0:T(8,128)}, u32[]{:S(2)}) %copy-start.1) | copy-done | bytes 2097176
  15.9 0.0 copy-start.4
  15.9 70.7 %factor_rows.1 = (f32[512,1024]{1,0:T(8,128)S(1)}, f32[512,1024]{1,0:T(8,128)S(1)}) custom-call(f32[1]{0:T(128)} %bitcast.1.live, f32[512,1024]{1,0:T(8,128)S(1)} %copy-done.1), custom_call_target="tpu_custom_call" | custom-call | flops 10000000000 | bytes 10000000 | tf_op jit(solution)/shard_map/factor_rows/pallas_call | solution.py:289
  86.6 0.0 copy-start.2
  86.6 1.3 copy-done.2
  88.0 42.2 %all-reduce.2.cloned.1.call-done.target = f32[512,1024]{1,0:T(8,128)} async-done(((f32[512,1024]{1,0:T(8,128)}), f32[512,1024]{1,0:T(8,128)}) %all-reduce.2.cloned.1.call-update) | async-done | bytes 2097168 | tf_op jit(solution)/shard_map/psum | solution.py:338
  130.1 0.0 copy-done.4
  130.1 0.0 copy-start
  130.1 1.6 %copy-done = f32[512,1024]{1,0:T(8,128)S(1)} copy-done((f32[512,1024]{1,0:T(8,128)S(1)}, f32[512,1024]{1,0:T(8,128)}, u32[]{:S(2)}) %copy-start) | copy-done | bytes 2097176
  131.7 0.0 copy-start.3
  131.7 2.8 %update_window.1 = f32[512,512]{1,0:T(8,128)} custom-call(f32[512,1024]{1,0:T(8,128)S(1)} %get-tuple-element.8.solved, f32[512,1024]{1,0:T(8,128)S(1)} %copy-done, f32[512,512]{1,0:T(8,128)S(1)} %copy-done.4), custom_call_target="tpu_custom_call" | custom-call | flops 1000000000 | bytes 10000000 | tf_op jit(solution)/shard_map/update_window/pallas_call | solution.py:320
  134.5 0.0 copy-done.3
  134.5 1.3 copy.8
Async XLA Ops:
  7.2 123.0 %all-reduce.2.cloned.1.call-start = ((), (), s32[]{:S(2)}) async-start(), calls=%async_computation | async-start | bytes 4194304 | tf_op jit(solution)/shard_map/psum | solution.py:338
  14.3 1.6 %copy-start.1 = (f32[512,1024]{1,0:T(8,128)S(1)}, f32[512,1024]{1,0:T(8,128)}, u32[]{:S(2)}) copy-start(f32[512,1024]{1,0:T(8,128)} %panel) | copy-start | bytes 6291460
  15.9 114.2 %copy-start.4 = (f32[512,512]{1,0:T(8,128)S(1)}, f32[512,512]{1,0:T(8,128)}, u32[]{:S(2)}) copy-start(f32[512,512]{1,0:T(8,128)} %window.1) | copy-start | bytes 3145732
  86.6 1.3 copy-start.2
  130.1 1.6 %copy-start = (f32[512,1024]{1,0:T(8,128)S(1)}, f32[512,1024]{1,0:T(8,128)}, u32[]{:S(2)}) copy-start(f32[512,1024]{1,0:T(8,128)} %all-reduce.2.cloned.1.call-done.target) | copy-start | bytes 6291460
  131.7 2.8 %copy-start.3 = (f32[512,1024]{1,0:T(8,128)S(1)}, f32[512,1024]{1,0:T(8,128)}, u32[]{:S(2)}) copy-start(f32[512,1024]{1,0:T(8,128)} %copy-done.2) | copy-start | bytes 6291460
Sparse Core Ops, SparseCore 0:
  14.4 115.6 all-reduce.1

commit v2 on v1

v2 whole, which is shorter than its diff:
```python
import functools

import jax
import jax.numpy as jnp
from jax import lax
from jax.experimental import pallas as pl
from jax.experimental.pallas import tpu as pltpu
from jax.sharding import PartitionSpec as P

P_SIZE = 2
HIGHEST = lax.Precision.HIGHEST
CONTRACT = (((1,), (1,)), ((), ()))
PLAIN = (((1,), (0,)), ((), ()))
LEAF = 128
GROUP = 16
WIDE = 256
MESH = pl.DeviceIdType.MESH


def halves(value):
    high = value.astype(jnp.bfloat16)
    return high, (value - high.astype(jnp.float32)).astype(jnp.bfloat16)


def product(left, right, contract):
    lh, ll = halves(left)
    rh, rl = halves(right)

    def dot(a, b):
        return lax.dot_general(a, b, contract, preferred_element_type=jnp.float32)

    return dot(lh, rh) + (dot(lh, rl) + dot(ll, rh))


def times_trans(left, right):
    return product(left, right, CONTRACT)


def times(left, right):
    return product(left, right, PLAIN)


def split3(value):
    high = value.astype(jnp.bfloat16).astype(jnp.float32)
    rest = value - high
    mid = rest.astype(jnp.bfloat16).astype(jnp.float32)
    return high, mid, rest - mid


def factor_leaf(aug, upper, inverse):
    lanes = lax.broadcasted_iota(jnp.int32, (GROUP, LEAF), 1)
    subs = lax.broadcasted_iota(jnp.int32, (GROUP, LEAF), 0)
    for g in range(LEAF // GROUP):
        base = g * GROUP
        left = aug[base : base + GROUP, :LEAF]
        right = aug[base : base + GROUP, LEAF:]
        cols = [
            jnp.broadcast_to(left[:, base + j : base + j + 1], (GROUP, LEAF)) for j in range(GROUP)
        ]
        scale = jnp.zeros((GROUP, LEAF), jnp.float32)
        for k in range(GROUP):
            pivot = jnp.broadcast_to(cols[k][k : k + 1, :], (GROUP, LEAF))
            root = lax.rsqrt(pivot)
            scale = jnp.where(subs == k, root, scale)
            if k + 1 < GROUP:
                mult = jnp.where(subs > k, cols[k] * (root * root), 0.0)
                for j in range(k + 1, GROUP):
                    cols[j] = cols[j] - mult * jnp.broadcast_to(cols[j][k : k + 1, :], (GROUP, LEAF))
                left = left - mult * jnp.broadcast_to(left[k : k + 1, :], (GROUP, LEAF))
                right = right - mult * jnp.broadcast_to(right[k : k + 1, :], (GROUP, LEAF))
        row_of = lanes - base
        left = jnp.where(row_of >= subs, left * scale, 0.0)
        right = right * scale
        upper[base : base + GROUP, :] = left
        inverse[base : base + GROUP, :] = right
        if base + GROUP < LEAF:
            lh, lm, ll = split3(left)
            rh, rm, rl = split3(right)
            keep = lanes >= base + GROUP
            a = [jnp.where(keep, v, 0.0) for v in (lh, lm, ll)]
            lhs = jnp.concatenate([a[0], a[0], a[1], a[0], a[1], a[2]], axis=0)
            rl_ = jnp.concatenate([lh, lm, lh, ll, lm, lh], axis=0)
            rr_ = jnp.concatenate([rh, rm, rh, rl, rm, rh], axis=0)
            rhs = jnp.concatenate([rl_, rr_], axis=1)
            update = lax.dot_general(
                lhs, rhs, (((0,), (0,)), ((), ())), preferred_element_type=jnp.float32)
            aug[base + GROUP :, :] = aug[base + GROUP :, :] - update[base + GROUP :, :]


CHUNKS = 4


class Traffic:
    def __init__(self, n_rows, n_cols, panel, own, lower, target, gathered, staged, sems):
        self.n_rows, self.n_cols = n_rows, n_cols
        self.n_pos = n_rows // 2
        self.r = lax.axis_index("rows")
        self.c = lax.axis_index("cols")
        self.q = lax.div(self.r, 2)
        self.p = lax.rem(self.r, 2)
        self.partner = self.r + 1 - 2 * self.p
        self.far = lax.rem(self.c + 2, 4)
        self.near = self.c + 1 - 2 * lax.rem(self.c, 2)
        self.panel, self.own, self.lower, self.target = panel, own, lower, target
        self.gathered, self.staged = gathered, staged
        (self.row_send, self.row_recv, self.far_send, self.far_recv, self.near_send, self.near_recv,
         self.dn_send, self.dn_recv, self.up_send, self.up_recv, self.x_send, self.x_recv,
         self.t_send, self.t_recv) = sems
        self.width = panel.shape[0]
        self.share = self.width // n_cols
        self.chunk = self.share // CHUNKS
        per = self.width // LEAF
        self.columns = []
        self.pieces = []
        for k in range(2 * per):
            column = []
            for which in range(2):
                lo = max(0, k - which * per) * LEAF
                if lo < self.width:
                    column.append(len(self.pieces))
                    self.pieces.append((which, lo, self.width - lo, k))
            self.columns.append(column)

    def barrier(self):
        sem = pltpu.get_barrier_semaphore()
        r, c, q = self.r, self.c, self.q

        def greet(row, col):
            pl.semaphore_signal(sem, inc=1, device_id=(row, col), device_id_type=MESH)

        for i in range(1, self.n_cols):
            greet(r, lax.rem(c + i, self.n_cols))
        greet(self.partner, c)

        @pl.when(q >= 1)
        def _():
            greet(r - 2, c)

        @pl.when(q + 1 < self.n_pos)
        def _():
            greet(r + 2, c)

        count = self.n_cols + (q >= 1).astype(jnp.int32) + (q + 1 < self.n_pos).astype(jnp.int32)
        pl.semaphore_wait(sem, count)

    def remote(self, src, dst, send, recv, row, col):
        return pltpu.make_async_remote_copy(
            src_ref=src, dst_ref=dst, send_sem=send, recv_sem=recv,
            device_id=(row, col), device_id_type=MESH)

    def place(self, ref, piece, owner):
        which, lo, size, k = self.pieces[piece]
        base = which * self.width if ref is self.lower else 0
        start = pl.multiple_of(base + lo + owner * (size // 4), 8)
        return ref.at[pl.ds(start, size // 4), pl.ds(k * LEAF, LEAF)]

    def to_row(self, piece, slot, dest, own):
        src = self.place(self.panel if own else self.lower, piece, self.c)
        return self.remote(src, self.place(self.lower, piece, self.c),
                           self.row_send.at[piece, slot], self.row_recv.at[piece], dest, self.c)

    def to_far(self, piece):
        spot = self.place(self.lower, piece, self.c)
        return self.remote(spot, spot, self.far_send.at[piece], self.far_recv.at[piece], self.r, self.far)

    def to_near(self, piece, slot):
        spot = self.place(self.lower, piece, (self.c, self.far)[slot])
        return self.remote(spot, spot, self.near_send.at[piece, slot], self.near_recv.at[piece, slot],
                           self.r, self.near)

    def send_diagonal(self):
        for piece, (which, _, _, _) in enumerate(self.pieces):

            @pl.when(self.r == which)
            def _():
                self.to_row(piece, 0, 1 - which, True).start()
                if which + 2 < self.n_rows:
                    self.to_row(piece, 1, which + 2, True).start()

    def column_in(self, k):
        for piece in self.columns[k]:

            @pl.when(self.r != self.pieces[piece][0])
            def _():
                self.to_row(piece, 0, self.r, False).wait_recv()

                @pl.when(self.r + 2 < self.n_rows)
                def _():
                    self.to_row(piece, 0, self.r + 2, False).start()

                self.to_far(piece).start()
                self.to_near(piece, 0).start()

    def column_far(self, k):
        for piece in self.columns[k]:

            @pl.when(self.r != self.pieces[piece][0])
            def _():
                self.to_far(piece).wait_recv()
                self.to_near(piece, 1).start()

    def column_done(self, k):
        for piece in self.columns[k]:
            which = self.pieces[piece][0]

            @pl.when(self.r != which)
            def _():
                for slot in range(2):
                    self.to_near(piece, slot).wait_recv()
                for slot in range(2):
                    self.to_near(piece, slot).wait_send()
                self.to_far(piece).wait_send()

                @pl.when(self.r + 2 < self.n_rows)
                def _():
                    self.to_row(piece, 0, self.r + 2, False).wait_send()

            @pl.when(self.r == which)
            def _():
                self.to_row(piece, 0, 1 - which, True).wait_send()
                if which + 2 < self.n_rows:
                    self.to_row(piece, 1, which + 2, True).wait_send()

    def part(self, ref, m):
        start = pl.multiple_of(self.c * self.share + m * self.chunk, 8)
        return ref.at[pl.ds(start, self.chunk), :]

    def gather(self, kind, s, m):
        q, p = self.q, self.p
        if kind == "dn":
            origin, dest, send, recv = q + s - 1, self.r - 2, self.dn_send, self.dn_recv
        else:
            origin, dest, send, recv = q - s + 1, self.r + 2, self.up_send, self.up_recv
        spot = self.gathered[m].at[2 * origin + p]
        src = self.part(self.panel, m) if s == 1 else spot
        return self.remote(src, spot, send.at[s - 1, m], recv.at[s - 1, m], dest, self.c)

    def awaited(self, kind, s, m):
        recv = self.dn_recv if kind == "dn" else self.up_recv
        send = self.dn_send if kind == "dn" else self.up_send
        row = self.r + 2 * s if kind == "dn" else self.r - 2 * s
        spot = self.gathered[m].at[row]
        return self.remote(spot, spot, send.at[s - 1, m], recv.at[s - 1, m], self.r, self.c)

    def across(self, origin, m, own):
        spot = self.gathered[m].at[2 * origin + self.p]
        src = self.part(self.panel, m) if own else spot
        return self.remote(src, spot, self.x_send.at[origin, m], self.x_recv.at[origin, m],
                           self.partner, self.c)

    def crossed(self, origin, m):
        spot = self.gathered[m].at[2 * origin + 1 - self.p]
        return self.remote(spot, spot, self.x_send.at[origin, m], self.x_recv.at[origin, m],
                           self.r, self.c)

    def open_down(self):
        @pl.when(self.q >= 1)
        def _():
            for m in range(CHUNKS):
                self.gather("dn", 1, m).start()
                self.across(self.q, m, True).start()

    def open_up(self):
        @pl.when((self.q >= 1) & (self.q + 1 < self.n_pos))
        def _():
            for m in range(CHUNKS):
                self.gather("up", 1, m).start()

    def round_down(self, s, m):
        if s < 1 or s > self.n_pos - 1:
            return

        @pl.when(self.q + s < self.n_pos)
        def _():
            self.awaited("dn", s, m).wait_recv()
            self.across(self.q + s, m, False).start()

            @pl.when(self.q >= 1)
            def _():
                self.gather("dn", s + 1, m).start()

    def round_up(self, s, m):
        if s < 1 or s > self.n_pos - 2:
            return

        @pl.when(self.q - s >= 1)
        def _():
            self.awaited("up", s, m).wait_recv()
            self.across(self.q - s, m, False).start()

            @pl.when(self.q + 1 < self.n_pos)
            def _():
                self.gather("up", s + 1, m).start()

    def keep_own(self):
        for m in range(CHUNKS):
            start = pl.multiple_of(self.c * self.share + m * self.chunk, 8)
            self.gathered[m][self.r] = self.own[pl.ds(start, self.chunk), :]

    def select(self, m, rows, live):
        for origin in range(1, self.n_pos):
            self.crossed(origin, m).wait_recv()
        start = pl.multiple_of(self.c * self.share + m * self.chunk, 8)
        for t in range(self.n_cols):
            value = self.gathered[m][rows[t]] * live[rows[t]].astype(jnp.float32)
            self.staged[m][t] = value

            @pl.when(self.c == t)
            def _():
                self.target[pl.ds(start, self.chunk), :] = value

    def deal(self, t, m):
        return self.remote(self.staged[m].at[t], self.part(self.target, m),
                           self.t_send.at[t, m], self.t_recv.at[self.c, m], self.r, t)

    def deal_all(self, m):
        for t in range(self.n_cols):

            @pl.when(self.c != t)
            def _():
                self.deal(t, m).start()

    def dealt(self, m):
        for i in range(1, self.n_cols):
            src = lax.rem(self.c + i, self.n_cols)
            start = pl.multiple_of(src * self.share + m * self.chunk, 8)
            spot = self.target.at[pl.ds(start, self.chunk), :]
            self.remote(spot, spot, self.t_send.at[src, m], self.t_recv.at[src, m], self.r, src).wait_recv()

    def finish(self):
        for m in range(CHUNKS):
            self.dealt(m)
            for t in range(self.n_cols):

                @pl.when(self.c != t)
                def _():
                    self.deal(t, m).wait_send()

            for s in range(1, self.n_pos):

                @pl.when((self.q >= 1) & (self.q + s - 1 < self.n_pos))
                def _():
                    self.gather("dn", s, m).wait_send()

                @pl.when((self.q + 1 < self.n_pos) & (self.q - s + 1 >= 1))
                def _():
                    self.gather("up", s, m).wait_send()

            for origin in range(1, self.n_pos):
                self.across(origin, m, False).wait_send()


def window_kernel(n_rows, n_cols, window_rows, row_live, panel, factor, solved, target,
                  own, lower, inverses, aug, upper, leaf_inv, *rest):
    gathered, staged = rest[:CHUNKS], rest[CHUNKS : 2 * CHUNKS]
    own_sem, sems = rest[2 * CHUNKS], rest[2 * CHUNKS + 1 :]
    net = Traffic(n_rows, n_cols, panel, own, lower, target, gathered, staged, sems)
    width = panel.shape[0]
    total = lower.shape[0]
    n_leaf = total // LEAF
    n_pos = n_rows // 2
    r = lax.axis_index("rows")
    fetch = pltpu.make_async_copy(panel, own, own_sem)
    fetch.start()
    net.barrier()
    net.send_diagonal()
    net.open_down()
    rows = lax.broadcasted_iota(jnp.int32, (LEAF, LEAF), 0)
    lanes = lax.broadcasted_iota(jnp.int32, (LEAF, LEAF), 1)
    inverses[...] = jnp.zeros(inverses.shape, jnp.float32)
    fetch.wait()

    @pl.when(r == 0)
    def _():
        lower[:width, :width] = own[:, :width]

    @pl.when(r == 1)
    def _():
        lower[width:, :] = own[...]

    for b in range(n_leaf - 1):
        lower[b * LEAF : (b + 1) * LEAF, (b + 1) * LEAF :] = jnp.zeros(
            (LEAF, total - (b + 1) * LEAF), jnp.float32)
    net.keep_own()
    net.column_in(0)
    net.column_in(1)
    net.column_far(0)
    net.column_far(1)
    net.column_in(2)
    net.column_done(0)
    net.open_up()
    for m in range(CHUNKS):
        for s in range(1, n_pos - 2):
            net.round_down(s, m)
            net.round_up(s - 1, m)

    def before(b):
        if b + 3 < n_leaf:
            net.column_in(b + 3)
        if b + 1 < n_leaf:
            net.column_done(b + 1)

    def after(b):
        if b + 2 < n_leaf:
            net.column_far(b + 2)
        half = [(0, 1), (2, 3)]
        if b in (1, 2):
            for m in half[b - 1]:
                net.round_down(n_pos - 2, m)
                net.round_up(n_pos - 3, m)
        if b in (3, 4):
            for m in half[b - 3]:
                net.round_down(n_pos - 1, m)
                net.round_up(n_pos - 2, m)

    def step(k, carry):
        at = pl.ds(pl.multiple_of(k * LEAF, LEAF), LEAF)
        block = lower[at, at]
        aug[:, :LEAF] = jnp.where(rows >= lanes, block, block.T)
        aug[:, LEAF:] = jnp.where(rows == lanes, 1.0, 0.0)
        factor_leaf(aug, upper, leaf_inv)
        lower[at, at] = upper[...].T
        for b in range(n_leaf):

            @pl.when(k == b)
            def _():
                before(b)
                if b in (5, 6):
                    for m in ((0, 1), (2, 3))[b - 5]:
                        net.select(m, window_rows, row_live)
                lo, hi = b * LEAF, (b + 1) * LEAF
                wide = b * LEAF // WIDE
                off = lo - wide * WIDE
                inv = leaf_inv[...]
                inverses[wide, off : off + LEAF, off : off + LEAF] = inv
                if off:
                    early = inverses[wide, :LEAF, :LEAF]
                    cross = lower[lo:hi, lo - LEAF : lo]
                    part = lax.dot_general(
                        cross, early, (((1,), (0,)), ((), ())), precision=HIGHEST,
                        preferred_element_type=jnp.float32)
                    inverses[wide, LEAF:, :LEAF] = -lax.dot_general(
                        inv, part, (((1,), (0,)), ((), ())), precision=HIGHEST,
                        preferred_element_type=jnp.float32)
                if hi < total:
                    lower[hi:, lo:hi] = times_trans(lower[hi:, lo:hi], inv)
                    nxt = hi + LEAF
                    lower[hi:, hi:nxt] = lower[hi:, hi:nxt] - times_trans(
                        lower[hi:, :hi], lower[hi:nxt, :hi])
                if b in (5, 6):
                    for m in ((0, 1), (2, 3))[b - 5]:
                        net.deal_all(m)
                after(b)

        return carry

    lax.fori_loop(0, n_leaf, step, 0)

    n_wide = total // WIDE
    live = jnp.where(r < P_SIZE, 1, row_live[r]).astype(jnp.float32)

    @pl.when(r < P_SIZE)
    def _():
        factor[...] = lower[pl.ds(pl.multiple_of(lax.rem(r, P_SIZE) * width, width), width), :]

    @pl.when(r >= P_SIZE)
    def _():
        factor[...] = own[...] * live
        for wide in range(n_wide):
            lo, hi = wide * WIDE, (wide + 1) * WIDE
            now = factor[:, lo:hi]
            if wide:
                now = now - times_trans(factor[:, :lo], lower[lo:hi, :lo])
            factor[:, lo:hi] = times_trans(now, inverses[wide])

    for wide in reversed(range(n_wide)):
        lo, hi = wide * WIDE, (wide + 1) * WIDE
        now = factor[:, lo:hi]
        if hi < total:
            now = now - times(solved[:, hi:], lower[hi:, lo:hi])
        solved[:, lo:hi] = times(now, inverses[wide])
    net.finish()


def factor_window(window_rows, row_live, panel, n_rows, n_cols):
    if n_cols != 4 or n_rows < 4 or n_rows % 2:
        raise ValueError("unsupported mesh")
    width, total = panel.shape
    n_leaf = total // LEAF
    n_pieces = n_leaf + width // LEAF
    n_pos = n_rows // 2
    chunk = width // n_cols // CHUNKS
    dma = pltpu.SemaphoreType.DMA
    return pl.pallas_call(
        functools.partial(window_kernel, n_rows, n_cols),
        out_shape=(jax.ShapeDtypeStruct(panel.shape, jnp.float32),) * 3,
        in_specs=[pl.BlockSpec(memory_space=pltpu.SMEM)] * 2 + [pl.BlockSpec(memory_space=pltpu.HBM)],
        out_specs=(pl.BlockSpec(memory_space=pltpu.VMEM),) * 3,
        scratch_shapes=[
            pltpu.VMEM(panel.shape, jnp.float32),
            pltpu.VMEM((total, total), jnp.float32),
            pltpu.VMEM((total // WIDE, WIDE, WIDE), jnp.float32),
            pltpu.VMEM((LEAF, 2 * LEAF), jnp.float32),
            pltpu.VMEM((LEAF, LEAF), jnp.float32),
            pltpu.VMEM((LEAF, LEAF), jnp.float32),
        ] + [pltpu.VMEM((n_rows, chunk, total), jnp.float32)] * CHUNKS
        + [pltpu.VMEM((n_cols, chunk, total), jnp.float32)] * CHUNKS
        + [
            dma(()),
            dma((n_pieces, 2)), dma((n_pieces,)), dma((n_pieces,)), dma((n_pieces,)),
            dma((n_pieces, 2)), dma((n_pieces, 2)),
            dma((n_pos, CHUNKS)), dma((n_pos, CHUNKS)), dma((n_pos, CHUNKS)), dma((n_pos, CHUNKS)),
            dma((n_pos, CHUNKS)), dma((n_pos, CHUNKS)),
            dma((n_cols, CHUNKS)), dma((n_cols, CHUNKS)),
        ],
        compiler_params=pltpu.CompilerParams(
            collective_id=0, has_side_effects=True, vmem_limit_bytes=(32 << 20) + n_rows * width * total * 4 // n_cols),
        cost_estimate=pl.CostEstimate(flops=10**10, bytes_accessed=10**7, transcendentals=0),
        name="factor_window",
    )(window_rows, row_live, panel)


def update_kernel(factor, solved, target, window, factor_out, updated, sem):
    store = pltpu.make_async_copy(factor, factor_out, sem)
    store.start()
    updated[...] = window[...] - times_trans(solved[...], target[...])
    store.wait()


def update_window(factor, solved, target, window):
    return pl.pallas_call(
        update_kernel,
        out_shape=(jax.ShapeDtypeStruct(factor.shape, jnp.float32),
                   jax.ShapeDtypeStruct(window.shape, jnp.float32)),
        in_specs=[pl.BlockSpec(memory_space=pltpu.VMEM)] * 4,
        out_specs=(pl.BlockSpec(memory_space=pltpu.HBM), pl.BlockSpec(memory_space=pltpu.VMEM)),
        scratch_shapes=[pltpu.SemaphoreType.DMA(())],
        compiler_params=pltpu.CompilerParams(vmem_limit_bytes=40 << 20),
        cost_estimate=pl.CostEstimate(flops=10**9, bytes_accessed=10**7, transcendentals=0),
        name="update_window",
    )(factor, solved, target, window)


def shards(n_rows, n_cols, panel, window_block, row_live, window_rows):
    factor, solved, target = factor_window(window_rows, row_live, panel, n_rows, n_cols)
    return update_window(factor, solved, target, window_block)


def solution(mesh):
    in_specs = (P("rows", None), P("rows", "cols"), P(), P())
    out_specs = (P("rows", None), P("rows", "cols"))
    body = functools.partial(shards, mesh.shape["rows"], mesh.shape["cols"])
    return jax.shard_map(body, mesh=mesh, in_specs=in_specs, out_specs=out_specs, check_vma=False)
```

time: 143 us -> 97.9 us (0.68)
  the two profiles are of different devices: /device:TPU:0 before, /device:TPU:27 now
where the time goes in v2:
time: 97.9 us; the launch traced here: 97.7 us
  Pallas kernels  93.9 us (96%)
  local copies, waits for them, and re-layouts  2.99 us (3%)
    pallas_call x1, Pallas kernels, factor_window(): pl.pallas_call(functools.partial(window_kernel, n_rows, n_cols), out_shap...  91.1 us
    unnamed x8, local copies, waits for them, and re-layouts  2.99 us
    pallas_call x1, Pallas kernels, update_window(): pl.pallas_call(update_kernel, out_shape=(jax.ShapeDtypeStruct(factor.shap...  2.81 us

profile of v2, /device:TPU:27, one launch (start us, length us, event | category | flops | bytes accessed | tf_op | source)
XLA Modules:
  0.0 97.7 jit_solution(795959715260151815)
XLA Ops:
  0.6 0.0 copy-start
  0.6 0.0 copy-start.1
  0.7 1.7 %copy-done.1 = f32[512,1024]{1,0:T(8,128)S(1)} copy-done((f32[512,1024]{1,0:T(8,128)S(1)}, f32[512,1024]{1,0:T(8,128)}, u32[]{:S(2)}) %copy-start.1) | copy-done | bytes 2097176
  2.3 0.0 copy-start.2
  2.3 0.7 copy-done.2
  3.0 0.0 copy-start.3
  3.0 0.7 copy-done.3
  3.6 91.1 %factor_window.1 = (f32[512,1024]{1,0:T(8,128)S(1)}, f32[512,1024]{1,0:T(8,128)S(1)}, f32[512,1024]{1,0:T(8,128)S(1)}) custom-call(s32[4]{0:T(128)S(1)} %copy-done.2, s32[8]{0:T(128)S(1)} %copy-done.3, f32[512,1024]{1,0:T(8,128)S(1)} %copy-done.1), custom_call_target="tpu_custom_call" | custom-call | flops 10000000000 | bytes 10000000 | tf_op jit(solution)/shard_map/factor_window/pallas_call | solution.py:494
  94.7 0.0 copy-done
  94.7 2.8 %update_window.1 = (f32[512,1024]{1,0:T(8,128)}, f32[512,512]{1,0:T(8,128)}) custom-call(f32[512,1024]{1,0:T(8,128)S(1)} %get-tuple-element.5.factor, f32[512,1024]{1,0:T(8,128)S(1)} %get-tuple-element.6.solved, f32[512,1024]{1,0:T(8,128)S(1)} %get-tuple-element.7.target, f32[512,512]{1,0:T(8,128)S(1)} %copy-done), custom_call_target="tpu_custom_call" | custom-call | flops 1000000000 | bytes 10000000 | tf_op jit(solution)/shard_map/update_window/pallas_call | solution.py:531
Async XLA Ops:
  0.6 94.1 %copy-start = (f32[512,512]{1,0:T(8,128)S(1)}, f32[512,512]{1,0:T(8,128)}, u32[]{:S(2)}) copy-start(f32[512,512]{1,0:T(8,128)} %window.1) | copy-start | bytes 3145732
  0.6 1.7 %copy-start.1 = (f32[512,1024]{1,0:T(8,128)S(1)}, f32[512,1024]{1,0:T(8,128)}, u32[]{:S(2)}) copy-start(f32[512,1024]{1,0:T(8,128)} %panel.1) | copy-start | bytes 6291460
  2.3 0.7 copy-start.2
  3.0 0.7 copy-start.3

commit v3 on v1

v3 whole, which is shorter than its diff:
```python
import functools

import jax
import jax.numpy as jnp
from jax import lax
from jax.experimental import pallas as pl
from jax.experimental.pallas import tpu as pltpu
from jax.sharding import PartitionSpec as P

P_SIZE = 2
CONTRACT = (((1,), (1,)), ((), ()))
LEAF = 128
GROUP = 16
CHUNKS = 4
MESH = pl.DeviceIdType.MESH


def halves(value):
    high = value.astype(jnp.bfloat16)
    return high, (value - high.astype(jnp.float32)).astype(jnp.bfloat16)


def product(left, right, contract):
    lh, ll = halves(left)
    rh, rl = halves(right)

    def dot(a, b):
        return lax.dot_general(a, b, contract, preferred_element_type=jnp.float32)

    return dot(lh, rh) + (dot(lh, rl) + dot(ll, rh))


def times_trans(left, right):
    return product(left, right, CONTRACT)


def split3(value):
    high = value.astype(jnp.bfloat16).astype(jnp.float32)
    rest = value - high
    mid = rest.astype(jnp.bfloat16).astype(jnp.float32)
    return high, mid, rest - mid


def factor_leaf(aug, upper, inverse):
    lanes = lax.broadcasted_iota(jnp.int32, (GROUP, LEAF), 1)
    subs = lax.broadcasted_iota(jnp.int32, (GROUP, LEAF), 0)
    for g in range(LEAF // GROUP):
        base = g * GROUP
        left = aug[base : base + GROUP, :LEAF]
        right = aug[base : base + GROUP, LEAF:]
        cols = [
            jnp.broadcast_to(left[:, base + j : base + j + 1], (GROUP, LEAF)) for j in range(GROUP)
        ]
        scale = jnp.zeros((GROUP, LEAF), jnp.float32)
        for k in range(GROUP):
            pivot = jnp.broadcast_to(cols[k][k : k + 1, :], (GROUP, LEAF))
            root = lax.rsqrt(pivot)
            scale = jnp.where(subs == k, root, scale)
            if k + 1 < GROUP:
                mult = jnp.where(subs > k, cols[k] * (root * root), 0.0)
                for j in range(k + 1, GROUP):
                    cols[j] = cols[j] - mult * jnp.broadcast_to(cols[j][k : k + 1, :], (GROUP, LEAF))
                left = left - mult * jnp.broadcast_to(left[k : k + 1, :], (GROUP, LEAF))
                right = right - mult * jnp.broadcast_to(right[k : k + 1, :], (GROUP, LEAF))
        row_of = lanes - base
        left = jnp.where(row_of >= subs, left * scale, 0.0)
        right = right * scale
        upper[base : base + GROUP, :] = left
        inverse[base : base + GROUP, :] = right
        if base + GROUP < LEAF:
            lh, lm, ll = split3(left)
            rh, rm, rl = split3(right)
            keep = lanes >= base + GROUP
            a = [jnp.where(keep, v, 0.0) for v in (lh, lm, ll)]
            lhs = jnp.concatenate([a[0], a[0], a[1], a[0], a[1], a[2]], axis=0)
            rl_ = jnp.concatenate([lh, lm, lh, ll, lm, lh], axis=0)
            rr_ = jnp.concatenate([rh, rm, rh, rl, rm, rh], axis=0)
            rhs = jnp.concatenate([rl_, rr_], axis=1)
            update = lax.dot_general(
                lhs, rhs, (((0,), (0,)), ((), ())), preferred_element_type=jnp.float32)
            aug[base + GROUP :, :] = aug[base + GROUP :, :] - update[base + GROUP :, :]


def remote(src, dst, send, recv, row, col):
    return pltpu.make_async_remote_copy(
        src_ref=src, dst_ref=dst, send_sem=send, recv_sem=recv,
        device_id=(row, col), device_id_type=MESH)


class Place:
    def __init__(self, n_rows, n_cols):
        self.n_rows, self.n_cols = n_rows, n_cols
        self.n_pos = n_rows // 2
        self.r = lax.axis_index("rows")
        self.c = lax.axis_index("cols")
        self.q = lax.div(self.r, 2)
        self.p = lax.rem(self.r, 2)
        self.partner = self.r + 1 - 2 * self.p
        self.far = lax.rem(self.c + 2, 4)
        self.near = self.c + 1 - 2 * lax.rem(self.c, 2)
        self.leads = self.q == 0
        self.follows = self.q >= 1
        self.passes = self.q + 1 < self.n_pos

    def barrier(self):
        sem = pltpu.get_barrier_semaphore()

        def greet(row, col):
            pl.semaphore_signal(sem, inc=1, device_id=(row, col), device_id_type=MESH)

        for i in range(1, self.n_cols):
            greet(self.r, lax.rem(self.c + i, self.n_cols))
        greet(self.partner, self.c)

        @pl.when(self.leads)
        def _():
            for s in range(1, self.n_pos):
                greet(self.r + 2 * s, self.c)
            pl.semaphore_wait(sem, self.n_cols + self.n_pos - 1)

        @pl.when(self.follows)
        def _():
            greet(self.p, self.c)

            @pl.when(self.q >= 2)
            def _():
                greet(self.r - 2, self.c)

            @pl.when(self.passes)
            def _():
                greet(self.r + 2, self.c)

            extra = (self.q >= 2).astype(jnp.int32) + self.passes.astype(jnp.int32)
            pl.semaphore_wait(sem, self.n_cols + 1 + extra)


class Blocks:
    def __init__(self, at, lower, pieces, sems):
        self.at, self.lower, self.pieces = at, lower, pieces
        (self.row_send, self.row_recv, self.far_send, self.far_recv, self.near_send, self.near_recv) = sems

    def of(self, k):
        return [i for i, piece in enumerate(self.pieces) if piece[3] == k]

    def place(self, piece, owner, ref=None, base=0):
        _, lo, size, k = self.pieces[piece]
        start = pl.multiple_of(lo - base + owner * (size // 4), 8)
        spot = (pl.ds(start, size // 4), pl.ds(k * LEAF, LEAF))
        return (self.lower if ref is None else ref).at[spot]

    def to_row(self, piece, slot, src=None):
        at = self.at
        spot = self.place(piece, at.c)
        return remote(spot if src is None else src, spot, self.row_send.at[piece, slot],
                      self.row_recv.at[piece], (at.r + 2, at.partner)[slot], at.c)

    def to_far(self, piece):
        at = self.at
        spot = self.place(piece, at.c)
        return remote(spot, spot, self.far_send.at[piece], self.far_recv.at[piece], at.r, at.far)

    def to_near(self, piece, slot):
        at = self.at
        spot = self.place(piece, (at.c, at.far)[slot])
        return remote(spot, spot, self.near_send.at[piece, slot], self.near_recv.at[piece, slot], at.r, at.near)

    def share(self, piece):
        self.to_far(piece).start()
        self.to_near(piece, 0).start()

    def share_far(self, piece):
        self.to_far(piece).wait_recv()
        self.to_near(piece, 1).start()

    def shared(self, piece):
        for slot in range(2):
            self.to_near(piece, slot).wait_recv()
        for slot in range(2):
            self.to_near(piece, slot).wait_send()
        self.to_far(piece).wait_send()


class Raw(Blocks):
    def send(self, panel, width):
        for piece, (which, _, _, _) in enumerate(self.pieces):

            @pl.when(self.at.r == which)
            def _():
                self.to_row(piece, 1, self.place(piece, self.at.c, panel, which * width)).start()

    def column(self, k, stage):
        for piece in self.of(k):
            which = self.pieces[piece][0]

            @pl.when(self.at.p != which)
            def _():
                if stage == 0:
                    self.to_row(piece, 1).wait_recv()
                    self.share(piece)
                elif stage == 1:
                    self.share_far(piece)
                else:
                    self.shared(piece)

            if stage == 2:

                @pl.when(self.at.p == which)
                def _():
                    self.to_row(piece, 1).wait_send()


class Solved(Blocks):
    def send(self, k):
        for piece in self.of(k):

            @pl.when(self.at.p == self.pieces[piece][0])
            def _():
                self.to_row(piece, 0).start()

    def sent(self, k):
        for piece in self.of(k):

            @pl.when(self.at.p == self.pieces[piece][0])
            def _():
                self.to_row(piece, 0).wait_send()

    def take(self, k):
        at = self.at
        for piece in self.of(k):

            @pl.when(at.p == self.pieces[piece][0])
            def _():
                self.to_row(piece, 0).wait_recv()

                @pl.when(at.passes)
                def _():
                    self.to_row(piece, 0).start()

                self.to_row(piece, 1).start()
                self.share(piece)

        for piece in self.of(k):

            @pl.when(at.p != self.pieces[piece][0])
            def _():
                self.to_row(piece, 1).wait_recv()
                self.share(piece)

    def take_far(self, k):
        for piece in self.of(k):
            self.share_far(piece)

    def taken(self, k):
        at = self.at
        for piece in self.of(k):
            self.shared(piece)

            @pl.when(at.p == self.pieces[piece][0])
            def _():
                self.to_row(piece, 1).wait_send()

                @pl.when(at.passes)
                def _():
                    self.to_row(piece, 0).wait_send()


class Rows:
    def __init__(self, at, panel, own, target, gathered, staged, sems):
        self.at, self.panel, self.own, self.target = at, panel, own, target
        self.gathered, self.staged = gathered, staged
        (self.dn_send, self.dn_recv, self.up_send, self.up_recv, self.x_send, self.x_recv,
         self.t_send, self.t_recv, self.l_send, self.l_recv) = sems
        self.width = panel.shape[0]
        self.share = self.width // at.n_cols
        self.chunk = self.share // CHUNKS

    def part(self, ref, m, owner=None):
        owner = self.at.c if owner is None else owner
        start = pl.multiple_of(owner * self.share + m * self.chunk, 8)
        return ref.at[pl.ds(start, self.chunk), :]

    def chain(self, kind, s, m):
        at = self.at
        if kind == "dn":
            origin, dest, send, recv = at.r + 2 * (s - 1), at.r - 2, self.dn_send, self.dn_recv
        else:
            origin, dest, send, recv = at.r - 2 * (s - 1), at.r + 2, self.up_send, self.up_recv
        spot = self.gathered[m].at[origin]
        src = self.part(self.panel, m) if s == 1 else spot
        return remote(src, spot, send.at[s - 1, m], recv.at[s - 1, m], dest, at.c)

    def awaited(self, kind, s, m):
        at = self.at
        recv, send = (self.dn_recv, self.dn_send) if kind == "dn" else (self.up_recv, self.up_send)
        spot = self.gathered[m].at[at.r + 2 * s if kind == "dn" else at.r - 2 * s]
        return remote(spot, spot, send.at[s - 1, m], recv.at[s - 1, m], at.r, at.c)

    def across(self, origin, m, own):
        at = self.at
        spot = self.gathered[m].at[2 * origin + at.p]
        src = self.part(self.panel, m) if own else spot
        return remote(src, spot, self.x_send.at[origin, m], self.x_recv.at[origin, m], at.partner, at.c)

    def crossed(self, origin, m):
        at = self.at
        spot = self.gathered[m].at[2 * origin + 1 - at.p]
        return remote(spot, spot, self.x_send.at[origin, m], self.x_recv.at[origin, m], at.r, at.c)

    def open(self):
        at = self.at
        for m in range(CHUNKS):

            @pl.when(at.q >= 2)
            def _():
                self.chain("dn", 1, m).start()

            @pl.when(at.passes)
            def _():
                self.chain("up", 1, m).start()

            self.across(at.q, m, True).start()

    def keep_own(self):
        for m in range(CHUNKS):
            start = pl.multiple_of(self.at.c * self.share + m * self.chunk, 8)
            self.gathered[m][self.at.r] = self.own[pl.ds(start, self.chunk), :]

    def relay(self, s, m):
        at = self.at

        @pl.when(at.q + s < at.n_pos)
        def _():
            self.awaited("dn", s, m).wait_recv()
            self.across(at.q + s, m, False).start()

            @pl.when(at.q >= 2)
            def _():
                self.chain("dn", s + 1, m).start()

        @pl.when(at.q - s >= 1)
        def _():
            self.awaited("up", s, m).wait_recv()
            self.across(at.q - s, m, False).start()

            @pl.when(at.passes)
            def _():
                self.chain("up", s + 1, m).start()

    def select(self, m, rows, live):
        at = self.at
        for origin in range(1, at.n_pos):
            self.crossed(origin, m).wait_recv()
        start = pl.multiple_of(at.c * self.share + m * self.chunk, 8)
        for t in range(at.n_cols):
            value = self.gathered[m][rows[t]] * live[rows[t]].astype(jnp.float32)
            self.staged[m][t] = value

            @pl.when(at.c == t)
            def _():
                self.target[pl.ds(start, self.chunk), :] = value

    def deal(self, t, m):
        at = self.at
        return remote(self.staged[m].at[t], self.part(self.target, m), self.t_send.at[t, m],
                      self.t_recv.at[at.c, m], at.r, t)

    def deal_all(self, m):
        for t in range(self.at.n_cols):

            @pl.when(self.at.c != t)
            def _():
                self.deal(t, m).start()

    def to_leader(self, owner, m):
        at = self.at
        start = pl.multiple_of(owner * self.share + m * self.chunk, 8)
        rows = pl.ds(start, self.chunk)
        src = self.target.at[rows, pl.ds(pl.multiple_of(at.p * self.width, LEAF), self.width)]
        return remote(src, self.target.at[rows, pl.ds(0, self.width)], self.l_send.at[owner, m],
                      self.l_recv.at[owner, m], at.p, at.c)

    def dealt(self, m):
        at = self.at
        for i in range(1, at.n_cols):
            src = lax.rem(at.c + i, at.n_cols)
            spot = self.part(self.target, m, src)
            remote(spot, spot, self.t_send.at[src, m], self.t_recv.at[src, m], at.r, src).wait_recv()

        @pl.when(at.q == 1)
        def _():
            for owner in range(at.n_cols):
                self.to_leader(owner, m).start()

    def arrived(self):
        for m in range(CHUNKS):
            for owner in range(self.at.n_cols):
                self.to_leader(owner, m).wait_recv()

    def finish(self):
        at = self.at
        for m in range(CHUNKS):
            for t in range(at.n_cols):

                @pl.when(at.c != t)
                def _():
                    self.deal(t, m).wait_send()

                @pl.when(at.q == 1)
                def _():
                    self.to_leader(t, m).wait_send()

            for s in range(1, at.n_pos - 1):

                @pl.when((at.q >= 2) & (at.q + s - 1 < at.n_pos))
                def _():
                    self.chain("dn", s, m).wait_send()

                @pl.when(at.passes & (at.q - s + 1 >= 1))
                def _():
                    self.chain("up", s, m).wait_send()

            for origin in range(1, at.n_pos):
                self.across(origin, m, False).wait_send()


def lead(at, raw, solved, send_inverse, own, lower, inverses, aug, upper):
    width = own.shape[0]
    total = lower.shape[0]
    n_leaf = total // LEAF
    rows = lax.broadcasted_iota(jnp.int32, (LEAF, LEAF), 0)
    lanes = lax.broadcasted_iota(jnp.int32, (LEAF, LEAF), 1)

    @pl.when(at.r == 0)
    def _():
        lower[:width, :width] = own[:, :width]

    @pl.when(at.r == 1)
    def _():
        lower[width:, :] = own[...]

    for b in range(n_leaf - 1):
        lower[b * LEAF : (b + 1) * LEAF, (b + 1) * LEAF :] = jnp.zeros(
            (LEAF, total - (b + 1) * LEAF), jnp.float32)
    raw.column(0, 0)
    raw.column(1, 0)
    raw.column(0, 1)
    raw.column(2, 0)
    raw.column(1, 1)
    raw.column(0, 2)

    def step(k, carry):
        here = pl.ds(pl.multiple_of(k * LEAF, LEAF), LEAF)
        block = lower[here, here]
        aug[:, :LEAF] = jnp.where(rows >= lanes, block, block.T)
        aug[:, LEAF:] = jnp.where(rows == lanes, 1.0, 0.0)
        factor_leaf(aug, upper, inverses.at[k])
        lower[here, here] = upper[...].T
        for b in range(n_leaf):

            @pl.when(k == b)
            def _():
                if b + 3 < n_leaf:
                    raw.column(b + 3, 0)
                if b + 2 < n_leaf:
                    raw.column(b + 2, 1)
                if b + 1 < n_leaf:
                    raw.column(b + 1, 2)
                lo, hi = b * LEAF, (b + 1) * LEAF
                send_inverse(b)
                if hi < total:
                    lower[hi:, lo:hi] = times_trans(lower[hi:, lo:hi], inverses[b])
                    nxt = hi + LEAF
                    lower[hi:, hi:nxt] = lower[hi:, hi:nxt] - times_trans(
                        lower[hi:, :hi], lower[hi:nxt, :hi])
                    solved.send(b)

        return carry

    lax.fori_loop(0, n_leaf, step, 0)


def window_kernel(n_rows, n_cols, rows_in, live_in, panel, window, factor, other, updated,
                  window_rows, row_live, own, lower, target, inverses, aug, upper, *rest):
    gathered, staged = rest[:CHUNKS], rest[CHUNKS : 2 * CHUNKS]
    own_sem, window_sem, rows_sem, live_sem = rest[2 * CHUNKS : 2 * CHUNKS + 4]
    sems = rest[2 * CHUNKS + 4 :]
    inv_send, inv_recv = sems[:2]
    at = Place(n_rows, n_cols)
    width = panel.shape[0]
    total = lower.shape[0]
    n_leaf = total // LEAF
    per = width // LEAF
    raw_pieces = [
        (which, which * width + max(0, k - which * per) * LEAF, width - max(0, k - which * per) * LEAF, k)
        for k in range(n_leaf) for which in range(2) if k < (which + 1) * per
    ]
    low_pieces = [
        (half, (k + 1) * LEAF + half * (total - (k + 1) * LEAF) // 2, (total - (k + 1) * LEAF) // 2, k)
        for k in range(n_leaf - 1) for half in range(2)
    ]
    raw = Raw(at, lower, raw_pieces, sems[2:8])
    solved = Solved(at, lower, low_pieces, sems[8:14])
    net = Rows(at, panel, own, target, gathered, staged, sems[14:])
    fetches = [
        pltpu.make_async_copy(panel, own, own_sem),
        pltpu.make_async_copy(window, updated, window_sem),
        pltpu.make_async_copy(rows_in, window_rows, rows_sem),
        pltpu.make_async_copy(live_in, row_live, live_sem),
    ]
    for fetch in fetches:
        fetch.start()
    at.barrier()

    def inverse(b, s):
        spot = inverses.at[b]
        return remote(spot, spot, inv_send.at[b, s - 1], inv_recv.at[b], at.r + 2 * s, at.c)

    def send_inverse(b):
        for s in reversed(range(1, at.n_pos)):
            inverse(b, s).start()

    @pl.when(at.leads)
    def _():
        raw.send(panel, width)

    @pl.when(at.follows)
    def _():
        net.open()

    for fetch in fetches:
        fetch.wait()
    live = row_live[at.r].astype(jnp.float32)

    @pl.when(at.leads)
    def _():
        lead(at, raw, solved, send_inverse, own, lower, inverses, aug, upper)
        factor[...] = lower[pl.ds(pl.multiple_of(at.p * width, width), width), :]
        for b in range(n_leaf):
            for s in range(1, at.n_pos):
                inverse(b, s).wait_send()
        for b in range(n_leaf - 1):
            solved.sent(b)
        net.arrived()
        updated[...] = updated[...] - target[:, :width].T

    @pl.when(at.follows)
    def _():
        net.keep_own()

        def ready(src, dst, b, scale):
            lo, hi = b * LEAF, (b + 1) * LEAF
            now = src[:, lo:hi]
            if scale is not None:
                now = now * scale
            if b:
                now = now - times_trans(dst[:, :lo], lower[lo:hi, :lo])
            dst[:, lo:hi] = now

        def close(dst, b):
            lo, hi = b * LEAF, (b + 1) * LEAF
            dst[:, lo:hi] = times_trans(dst[:, lo:hi], inverses[b])

        for b in range(n_leaf):
            if b == 1:
                for s in range(1, at.n_pos - 2):
                    for m in range(CHUNKS):
                        net.relay(s, m)
            if b in (2, 3) and at.n_pos > 2:
                for m in ((0, 1), (2, 3))[b - 2]:
                    net.relay(at.n_pos - 2, m)
            if 3 <= b < 3 + CHUNKS:
                net.select(b - 3, window_rows, row_live)
            if b:
                solved.take(b - 1)
                solved.take_far(b - 1)
            if 3 <= b < 3 + CHUNKS:
                net.deal_all(b - 3)
            if 5 <= b < 5 + CHUNKS:
                net.dealt(b - 5)
            if b:
                solved.taken(b - 1)
            ready(own, factor, b, live)
            if b == n_leaf - 1:
                net.dealt(CHUNKS - 1)
                for k in range(b):
                    ready(target, other, k, None)
                    close(other, k)
                ready(target, other, b, None)
                lo = b * LEAF
                updated[...] = updated[...] - times_trans(factor[:, :lo], other[:, :lo])
            inverse(b, 0).wait_recv()
            close(factor, b)
        close(other, n_leaf - 1)
        net.finish()


def factor_window(window_rows, row_live, panel, window, n_rows, n_cols):
    if n_cols != 4 or n_rows < 6 or n_rows % 2:
        raise ValueError("unsupported mesh")
    width, total = panel.shape
    n_leaf = total // LEAF
    n_raw = n_leaf + width // LEAF
    n_low = 2 * (n_leaf - 1)
    n_pos = n_rows // 2
    chunk = width // n_cols // CHUNKS
    dma = pltpu.SemaphoreType.DMA
    tall = jax.ShapeDtypeStruct(panel.shape, jnp.float32)
    return pl.pallas_call(
        functools.partial(window_kernel, n_rows, n_cols),
        out_shape=(tall, tall, jax.ShapeDtypeStruct(window.shape, jnp.float32)),
        in_specs=[pl.BlockSpec(memory_space=pltpu.HBM)] * 4,
        out_specs=(pl.BlockSpec(memory_space=pltpu.VMEM),) * 3,
        scratch_shapes=[
            pltpu.SMEM(window_rows.shape, jnp.int32),
            pltpu.SMEM(row_live.shape, jnp.int32),
            pltpu.VMEM(panel.shape, jnp.float32),
            pltpu.VMEM((total, total), jnp.float32),
            pltpu.VMEM(panel.shape, jnp.float32),
            pltpu.VMEM((n_leaf, LEAF, LEAF), jnp.float32),
            pltpu.VMEM((LEAF, 2 * LEAF), jnp.float32),
            pltpu.VMEM((LEAF, LEAF), jnp.float32),
        ] + [pltpu.VMEM((n_rows, chunk, total), jnp.float32)] * CHUNKS
        + [pltpu.VMEM((n_cols, chunk, total), jnp.float32)] * CHUNKS
        + [
            dma(()), dma(()), dma(()), dma(()),
            dma((n_leaf, n_pos - 1)), dma((n_leaf,)),
            dma((n_raw, 2)), dma((n_raw,)), dma((n_raw,)), dma((n_raw,)), dma((n_raw, 2)), dma((n_raw, 2)),
            dma((n_low, 2)), dma((n_low,)), dma((n_low,)), dma((n_low,)), dma((n_low, 2)), dma((n_low, 2)),
            dma((n_pos, CHUNKS)), dma((n_pos, CHUNKS)), dma((n_pos, CHUNKS)), dma((n_pos, CHUNKS)),
            dma((n_pos, CHUNKS)), dma((n_pos, CHUNKS)),
            dma((n_cols, CHUNKS)), dma((n_cols, CHUNKS)), dma((n_cols, CHUNKS)), dma((n_cols, CHUNKS)),
        ],
        compiler_params=pltpu.CompilerParams(
            collective_id=0, has_side_effects=True, vmem_limit_bytes=(21 << 20) + n_rows * n_cols * CHUNKS * chunk * total),
        cost_estimate=pl.CostEstimate(flops=10**10, bytes_accessed=10**7, transcendentals=0),
        name="factor_window",
    )(*[pltpu.with_memory_space_constraint(x, pltpu.HBM) for x in (window_rows, row_live, panel, window)])


def update_kernel(factor, other, partial, factor_out, updated, sem):
    store = pltpu.make_async_copy(factor, factor_out, sem)
    store.start()
    r = lax.axis_index("rows")
    lo = factor.shape[1] - LEAF

    @pl.when(r < P_SIZE)
    def _():
        updated[...] = partial[...]

    @pl.when(r >= P_SIZE)
    def _():
        updated[...] = partial[...] - times_trans(factor[:, lo:], other[:, lo:])

    store.wait()


def update_window(factor, other, partial):
    return pl.pallas_call(
        update_kernel,
        out_shape=(jax.ShapeDtypeStruct(factor.shape, jnp.float32),
                   jax.ShapeDtypeStruct(partial.shape, jnp.float32)),
        in_specs=[pl.BlockSpec(memory_space=pltpu.VMEM)] * 3,
        out_specs=(pl.BlockSpec(memory_space=pltpu.HBM), pl.BlockSpec(memory_space=pltpu.VMEM)),
        scratch_shapes=[pltpu.SemaphoreType.DMA(())],
        compiler_params=pltpu.CompilerParams(vmem_limit_bytes=24 << 20),
        cost_estimate=pl.CostEstimate(flops=10**9, bytes_accessed=10**7, transcendentals=0),
        name="update_window",
    )(factor, other, partial)


def shards(n_rows, n_cols, panel, window_block, row_live, window_rows):
    factor, other, partial = factor_window(window_rows, row_live, panel, window_block, n_rows, n_cols)
    return update_window(factor, other, partial)


def solution(mesh):
    in_specs = (P("rows", None), P("rows", "cols"), P(), P())
    out_specs = (P("rows", None), P("rows", "cols"))
    body = functools.partial(shards, mesh.shape["rows"], mesh.shape["cols"])
    return jax.shard_map(body, mesh=mesh, in_specs=in_specs, out_specs=out_specs, check_vma=False)
```

time: 143 us -> 125 us (0.87)
  the two profiles are of different devices: /device:TPU:0 before, /device:TPU:27 now
where the time goes in v3:
time: 125 us; the launch traced here: 124 us
  Pallas kernels  123 us (98%)
    pallas_call x1, Pallas kernels, factor_window(): pl.pallas_call(functools.partial(window_kernel, n_rows, n_cols), out_shap...  121 us

profile of v3, /device:TPU:27, one launch (start us, length us, event | category | flops | bytes accessed | tf_op | source)
XLA Modules:
  0.0 124.1 jit_solution(17648732408881212770)
XLA Ops:
  0.6 121.0 %factor_window.1 = (f32[512,1024]{1,0:T(8,128)S(1)}, f32[512,1024]{1,0:T(8,128)S(1)}, f32[512,512]{1,0:T(8,128)S(1)}) custom-call(s32[4]{0:T(128)} %rows_in.1, s32[8]{0:T(128)} %live_in.1, f32[512,1024]{1,0:T(8,128)} %panel.1, f32[512,512]{1,0:T(8,128)} %window.1), custom_call_target="tpu_custom_call" | custom-call | flops 10000000000 | bytes 10000000 | tf_op jit(solution)/shard_map/factor_window/pallas_call | solution.py:608
  121.6 2.3 %update_window.1 = (f32[512,1024]{1,0:T(8,128)}, f32[512,512]{1,0:T(8,128)}) custom-call(f32[512,1024]{1,0:T(8,128)S(1)} %get-tuple-element.5.factor, f32[512,1024]{1,0:T(8,128)S(1)} %get-tuple-element.6.other, f32[512,512]{1,0:T(8,128)S(1)} %get-tuple-element.7.partial), custom_call_target="tpu_custom_call" | custom-call | flops 1000000000 | bytes 10000000 | tf_op jit(solution)/shard_map/update_window/pallas_call | solution.py:658

commit v4 on v3

v4 whole, which is shorter than its diff:
```python
import functools

import jax
import jax.numpy as jnp
from jax import lax
from jax.experimental import pallas as pl
from jax.experimental.pallas import tpu as pltpu
from jax.sharding import PartitionSpec as P

P_SIZE = 2
CONTRACT = (((1,), (1,)), ((), ()))
LEAF = 128
GROUP = 16
CHUNKS = 4
MESH = pl.DeviceIdType.MESH


def halves(value):
    high = value.astype(jnp.bfloat16)
    return high, (value - high.astype(jnp.float32)).astype(jnp.bfloat16)


def product(left, right):
    (lh, ll), (rh, rl) = left, right

    def dot(a, b):
        return lax.dot_general(a, b, CONTRACT, preferred_element_type=jnp.float32)

    return dot(lh, rh) + (dot(lh, rl) + dot(ll, rh))


def times_trans(left, right):
    return product(halves(left), halves(right))


class Split:
    def __init__(self, high, low):
        self.high, self.low = high, low

    def put(self, rows, cols, value):
        self.high[rows, cols], self.low[rows, cols] = halves(value)

    def get(self, rows, cols):
        return self.high[rows, cols], self.low[rows, cols]


def spread_row(value, k):
    return jnp.broadcast_to(value[k : k + 1, :], value.shape)


def factor_leaf(aug, upper, inverse):
    half = GROUP // 2
    subs = lax.broadcasted_iota(jnp.int32, (half, LEAF), 0)
    row_of = lax.broadcasted_iota(jnp.int32, (GROUP, LEAF), 1) - lax.broadcasted_iota(jnp.int32, (GROUP, LEAF), 0)
    lanes = lax.broadcasted_iota(jnp.int32, (GROUP, LEAF), 1)
    for g in range(LEAF // GROUP):
        base = g * GROUP
        parts = [[aug[base + h * half : base + (h + 1) * half, s * LEAF : (s + 1) * LEAF] for s in range(2)]
                 for h in range(2)]
        cols = [[jnp.broadcast_to(parts[h][0][:, base + j : base + j + 1], (half, LEAF)) for j in range(GROUP)]
                for h in range(2)]
        scales = [jnp.zeros((half, LEAF), jnp.float32)] * 2
        for k in range(GROUP):
            h, kk = k // half, k % half
            root = lax.rsqrt(spread_row(cols[h][k], kk))
            scales[h] = jnp.where(subs == kk, root, scales[h])
            if k + 1 == GROUP:
                break
            inv = root * root
            mults = {i: cols[i][k] * inv for i in range(h, 2)}
            for j in range(k + 1, GROUP):
                row = spread_row(cols[h][j], kk)
                for i in range(h, 2):
                    cols[i][j] = cols[i][j] - mults[i] * row
            mults[h] = jnp.where(subs > kk, mults[h], 0.0)
            for s in range(2):
                row = spread_row(parts[h][s], kk)
                for i in range(h, 2):
                    parts[i][s] = parts[i][s] - mults[i] * row
        left = jnp.concatenate([parts[h][0] * scales[h] for h in range(2)], axis=0)
        right = jnp.concatenate([parts[h][1] * scales[h] for h in range(2)], axis=0)
        left = jnp.where(row_of >= base, left, 0.0)
        upper[base : base + GROUP, :] = left
        inverse[base : base + GROUP, :] = right
        if base + GROUP < LEAF:
            both = jnp.concatenate([left, right], axis=1)
            high = both.astype(jnp.bfloat16).astype(jnp.float32)
            low = both - high
            keep = lanes >= base + GROUP
            lh, ll = [jnp.where(keep, v[:, :LEAF], 0.0) for v in (high, low)]
            update = lax.dot_general(
                jnp.concatenate([lh, ll, lh], axis=0), jnp.concatenate([high, high, low], axis=0),
                (((0,), (0,)), ((), ())), preferred_element_type=jnp.float32)
            aug[base + GROUP :, :] = aug[base + GROUP :, :] - update[base + GROUP :, :]


def remote(src, dst, send, recv, row, col):
    return pltpu.make_async_remote_copy(
        src_ref=src, dst_ref=dst, send_sem=send, recv_sem=recv,
        device_id=(row, col), device_id_type=MESH)


class Place:
    def __init__(self, n_rows, n_cols):
        self.n_rows, self.n_cols = n_rows, n_cols
        self.n_pos = n_rows // 2
        self.r = lax.axis_index("rows")
        self.c = lax.axis_index("cols")
        self.q = lax.div(self.r, 2)
        self.p = lax.rem(self.r, 2)
        self.partner = self.r + 1 - 2 * self.p
        self.far = lax.rem(self.c + 2, 4)
        self.near = self.c + 1 - 2 * lax.rem(self.c, 2)
        self.leads = self.q == 0
        self.follows = self.q >= 1
        self.passes = self.q + 1 < self.n_pos

    def barrier(self):
        sem = pltpu.get_barrier_semaphore()

        def greet(row, col):
            pl.semaphore_signal(sem, inc=1, device_id=(row, col), device_id_type=MESH)

        for i in range(1, self.n_cols):
            greet(self.r, lax.rem(self.c + i, self.n_cols))
        greet(self.partner, self.c)

        @pl.when(self.leads)
        def _():
            for s in range(1, self.n_pos):
                greet(self.r + 2 * s, self.c)
            pl.semaphore_wait(sem, self.n_cols + self.n_pos - 1)

        @pl.when(self.follows)
        def _():
            greet(self.p, self.c)

            @pl.when(self.q >= 2)
            def _():
                greet(self.r - 2, self.c)

            @pl.when(self.passes)
            def _():
                greet(self.r + 2, self.c)

            extra = (self.q >= 2).astype(jnp.int32) + self.passes.astype(jnp.int32)
            pl.semaphore_wait(sem, self.n_cols + 1 + extra)


class Blocks:
    def __init__(self, at, lower, pieces, sems):
        self.at, self.lower, self.pieces = at, lower, pieces
        self.row_send, self.row_recv, self.near_send, self.near_recv = sems

    def of(self, k):
        return [i for i, piece in enumerate(self.pieces) if piece[3] == k]

    def half(self, piece, owner):
        _, lo, size, k = self.pieces[piece]
        start = pl.multiple_of(lo + owner * (size // 2), 8)
        return self.lower.at[k, pl.ds(start, size // 2), :]

    def place(self, piece):
        return self.half(piece, lax.rem(self.at.c, 2))

    def to_row(self, piece, row):
        spot = self.place(piece)
        return remote(spot, spot, self.row_send.at[piece], self.row_recv.at[piece], row, self.at.c)

    def to_near(self, piece):
        spot = self.place(piece)
        return remote(spot, spot, self.near_send.at[piece], self.near_recv.at[piece], self.at.r, self.at.near)

    def near_in(self, piece):
        spot = self.half(piece, 1 - lax.rem(self.at.c, 2))
        return remote(spot, spot, self.near_send.at[piece], self.near_recv.at[piece], self.at.r, self.at.near)


class Raw(Blocks):
    def send(self, k):
        for piece in self.of(k):

            @pl.when(self.at.r == self.pieces[piece][0])
            def _():
                self.to_row(piece, self.at.partner).start()

    def come(self, piece):
        @pl.when(self.at.p != self.pieces[piece][0])
        def _():
            self.to_row(piece, self.at.partner).wait_recv()
            self.to_near(piece).start()

    def done(self, piece):
        @pl.when(self.at.p != self.pieces[piece][0])
        def _():
            self.near_in(piece).wait_recv()
            self.to_near(piece).wait_send()

        @pl.when(self.at.p == self.pieces[piece][0])
        def _():
            self.to_row(piece, self.at.partner).wait_send()


class Solved(Blocks):
    def __init__(self, at, lower, pieces, sems, straight=None):
        super().__init__(at, lower, pieces, sems)
        self.straight = straight

    def is_last(self, piece):
        return self.straight is not None and piece + 1 == len(self.pieces)

    def sends(self, piece):
        if not self.is_last(piece):
            return [self.to_row(piece, self.at.r + 2)]
        spot = self.place(piece)
        return [
            remote(spot, spot, self.straight.at[s - 1], self.row_recv.at[piece], self.at.r + 2 * s, self.at.c)
            for s in reversed(range(1, self.at.n_pos))
        ]

    def send(self, piece):
        for copy in self.sends(piece):
            copy.start()

    def sent(self, piece):
        for copy in self.sends(piece):
            copy.wait_send()

    def take(self, piece):
        self.to_row(piece, self.at.r + 2).wait_recv()
        if not self.is_last(piece):

            @pl.when(self.at.passes)
            def _():
                self.to_row(piece, self.at.r + 2).start()

        self.to_near(piece).start()

    def taken(self, piece):
        self.near_in(piece).wait_recv()

    def finish(self):
        for piece in range(len(self.pieces)):
            self.to_near(piece).wait_send()
            if not self.is_last(piece):

                @pl.when(self.at.passes)
                def _():
                    self.to_row(piece, self.at.r + 2).wait_send()


class Rows:
    def __init__(self, at, panel, own, target, gathered, staged, sems):
        self.at, self.panel, self.own, self.target = at, panel, own, target
        self.gathered, self.staged = gathered, staged
        (self.dn_send, self.dn_recv, self.up_send, self.up_recv, self.x_send, self.x_recv,
         self.t_send, self.t_recv, self.l_send, self.l_recv) = sems
        self.width = panel.shape[0]
        self.share = self.width // at.n_cols
        self.chunk = self.share // CHUNKS

    def part(self, ref, m, owner=None):
        owner = self.at.c if owner is None else owner
        start = pl.multiple_of(owner * self.share + m * self.chunk, 8)
        return ref.at[pl.ds(start, self.chunk), :]

    def chain(self, kind, s, m):
        at = self.at
        if kind == "dn":
            origin, dest, send, recv = at.r + 2 * (s - 1), at.r - 2, self.dn_send, self.dn_recv
        else:
            origin, dest, send, recv = at.r - 2 * (s - 1), at.r + 2, self.up_send, self.up_recv
        spot = self.gathered[m].at[origin]
        src = self.part(self.panel, m) if s == 1 else spot
        return remote(src, spot, send.at[s - 1, m], recv.at[s - 1, m], dest, at.c)

    def awaited(self, kind, s, m):
        at = self.at
        recv, send = (self.dn_recv, self.dn_send) if kind == "dn" else (self.up_recv, self.up_send)
        spot = self.gathered[m].at[at.r + 2 * s if kind == "dn" else at.r - 2 * s]
        return remote(spot, spot, send.at[s - 1, m], recv.at[s - 1, m], at.r, at.c)

    def across(self, origin, m, own):
        at = self.at
        spot = self.gathered[m].at[2 * origin + at.p]
        src = self.part(self.panel, m) if own else spot
        return remote(src, spot, self.x_send.at[origin, m], self.x_recv.at[origin, m], at.partner, at.c)

    def crossed(self, origin, m):
        at = self.at
        spot = self.gathered[m].at[2 * origin + 1 - at.p]
        return remote(spot, spot, self.x_send.at[origin, m], self.x_recv.at[origin, m], at.r, at.c)

    def open(self):
        at = self.at
        for m in range(CHUNKS):

            @pl.when(at.q >= 2)
            def _():
                self.chain("dn", 1, m).start()

            @pl.when(at.passes)
            def _():
                self.chain("up", 1, m).start()

            self.across(at.q, m, True).start()

    def keep_own(self):
        for m in range(CHUNKS):
            start = pl.multiple_of(self.at.c * self.share + m * self.chunk, 8)
            self.gathered[m][self.at.r] = self.own[pl.ds(start, self.chunk), :]

    def relay(self, s, m):
        at = self.at

        @pl.when(at.q + s < at.n_pos)
        def _():
            self.awaited("dn", s, m).wait_recv()
            self.across(at.q + s, m, False).start()

            @pl.when(at.q >= 2)
            def _():
                self.chain("dn", s + 1, m).start()

        @pl.when(at.q - s >= 1)
        def _():
            self.awaited("up", s, m).wait_recv()
            self.across(at.q - s, m, False).start()

            @pl.when(at.passes)
            def _():
                self.chain("up", s + 1, m).start()

    def select(self, m, rows, live):
        at = self.at
        for origin in range(1, at.n_pos):
            self.crossed(origin, m).wait_recv()
        start = pl.multiple_of(at.c * self.share + m * self.chunk, 8)
        for t in range(at.n_cols):
            value = self.gathered[m][rows[t]] * live[rows[t]].astype(jnp.float32)
            self.staged[m][t] = value

            @pl.when(at.c == t)
            def _():
                self.target[pl.ds(start, self.chunk), :] = value

    def deal(self, t, m):
        at = self.at
        return remote(self.staged[m].at[t], self.part(self.target, m), self.t_send.at[t, m],
                      self.t_recv.at[at.c, m], at.r, t)

    def deal_all(self, m):
        for t in range(self.at.n_cols):

            @pl.when(self.at.c != t)
            def _():
                self.deal(t, m).start()

    def to_leader(self, owner, m):
        at = self.at
        start = pl.multiple_of(owner * self.share + m * self.chunk, 8)
        rows = pl.ds(start, self.chunk)
        src = self.target.at[rows, pl.ds(pl.multiple_of(at.p * self.width, LEAF), self.width)]
        return remote(src, self.target.at[rows, pl.ds(0, self.width)], self.l_send.at[owner, m],
                      self.l_recv.at[owner, m], at.p, at.c)

    def dealt(self, m):
        at = self.at
        for i in range(1, at.n_cols):
            src = lax.rem(at.c + i, at.n_cols)
            spot = self.part(self.target, m, src)
            remote(spot, spot, self.t_send.at[src, m], self.t_recv.at[src, m], at.r, src).wait_recv()

        @pl.when(at.q == 1)
        def _():
            for owner in range(at.n_cols):
                self.to_leader(owner, m).start()

    def arrived(self):
        for m in range(CHUNKS):
            for owner in range(self.at.n_cols):
                self.to_leader(owner, m).wait_recv()

    def finish(self):
        at = self.at
        for m in range(CHUNKS):
            for t in range(at.n_cols):

                @pl.when(at.c != t)
                def _():
                    self.deal(t, m).wait_send()

                @pl.when(at.q == 1)
                def _():
                    self.to_leader(t, m).wait_send()

            for s in range(1, at.n_pos - 1):

                @pl.when((at.q >= 2) & (at.q + s - 1 < at.n_pos))
                def _():
                    self.chain("dn", s, m).wait_send()

                @pl.when(at.passes & (at.q - s + 1 >= 1))
                def _():
                    self.chain("up", s, m).wait_send()

            for origin in range(1, at.n_pos):
                self.across(origin, m, False).wait_send()


def lead(at, raw, solved, inverted, lower, split, inverses, aug, upper):
    total = lower.shape[1]
    n_leaf = total // LEAF
    rows = lax.broadcasted_iota(jnp.int32, (LEAF, LEAF), 0)
    lanes = lax.broadcasted_iota(jnp.int32, (LEAF, LEAF), 1)

    for b in range(1, n_leaf):
        lower[b, : b * LEAF, :] = jnp.zeros((b * LEAF, LEAF), jnp.float32)
    first = raw.of(0)
    raw.come(first[0])
    raw.done(first[0])

    def step(k, carry):
        here = pl.ds(pl.multiple_of(k * LEAF, LEAF), LEAF)
        block = lower[k, here, :]
        aug[:, :LEAF] = jnp.where(rows >= lanes, block, block.T)
        aug[:, LEAF:] = jnp.where(rows == lanes, 1.0, 0.0)
        factor_leaf(aug, upper, inverses.at[k])
        lower[k, here, :] = upper[...].T
        for b in range(n_leaf):

            @pl.when(k == b)
            def _():
                inverted.send(b)
                if b == 0:
                    for piece in first[1:] + raw.of(1) + raw.of(2):
                        raw.come(piece)
                    for piece in first[1:] + raw.of(1):
                        raw.done(piece)
                else:
                    if b + 2 < n_leaf:
                        for piece in raw.of(b + 2):
                            raw.come(piece)
                    if b + 1 < n_leaf:
                        for piece in raw.of(b + 1):
                            raw.done(piece)
                lo, hi = b * LEAF, (b + 1) * LEAF
                if hi < total:
                    column = times_trans(lower[b, hi:, :], inverses[b])
                    lower[b, hi:, :] = column
                    split.put(slice(hi, total), slice(lo, hi), column)
                    nxt = hi + LEAF
                    lower[b + 1, hi:, :] = lower[b + 1, hi:, :] - product(
                        split.get(slice(hi, total), slice(0, hi)), split.get(slice(hi, nxt), slice(0, hi)))
                    solved.send(b)

        return carry

    lax.fori_loop(0, n_leaf, step, 0)


def window_kernel(n_rows, n_cols, rows_in, live_in, panel, window, factor, other, updated,
                  window_rows, row_live, own, lower, target, inverses, aug, upper,
                  low_high, low_low, x_high, x_low, j_high, j_low, *rest):
    gathered, staged = rest[:CHUNKS], rest[CHUNKS : 2 * CHUNKS]
    own_sem, window_sem, rows_sem, live_sem, block_sem = rest[2 * CHUNKS : 2 * CHUNKS + 5]
    sems = rest[2 * CHUNKS + 5 :]
    at = Place(n_rows, n_cols)
    width = panel.shape[0]
    total = lower.shape[1]
    n_leaf = total // LEAF
    per = width // LEAF
    raw_pieces = [(0, 0, LEAF, 0), (0, LEAF, width - LEAF, 0)] + [
        (which, which * width + max(0, k - which * per) * LEAF, width - max(0, k - which * per) * LEAF, k)
        for k in range(n_leaf) for which in range(2) if k < (which + 1) * per and (k, which) != (0, 0)
    ]
    low_pieces = [(0, (k + 1) * LEAF, total - (k + 1) * LEAF, k) for k in range(n_leaf - 1)]
    raw = Raw(at, lower, raw_pieces, sems[1:5])
    solved = Solved(at, lower, low_pieces, sems[5:9])
    inv_pieces = [(0, 0, LEAF, k) for k in range(n_leaf)]
    inverted = Solved(at, inverses, inv_pieces, sems[9:13], sems[0])
    low_split, x_split = Split(low_high, low_low), Split(x_high, x_low)
    net = Rows(at, panel, own, target, gathered, staged, sems[13:])
    fetches = [
        pltpu.make_async_copy(window, updated, window_sem),
        pltpu.make_async_copy(rows_in, window_rows, rows_sem),
        pltpu.make_async_copy(live_in, row_live, live_sem),
    ]
    keep = pltpu.make_async_copy(panel, own, own_sem)

    def block_fetch(k):
        return pltpu.make_async_copy(
            panel.at[:, pl.ds(k * LEAF, LEAF)],
            lower.at[k, pl.ds(pl.multiple_of(at.p * width, LEAF), width), :], block_sem.at[k])

    @pl.when(at.leads)
    def _():
        for k in range(n_leaf):

            @pl.when(k < (at.p + 1) * per)
            def _():
                block_fetch(k).start()

    @pl.when(at.follows)
    def _():
        keep.start()

    for fetch in fetches:
        fetch.start()
    at.barrier()

    @pl.when(at.follows)
    def _():
        net.open()
        keep.wait()

    @pl.when(at.leads)
    def _():
        for k in range(n_leaf):

            @pl.when(k < (at.p + 1) * per)
            def _():
                block_fetch(k).wait()
                raw.send(k)

    for fetch in fetches:
        fetch.wait()
    live = row_live[at.r].astype(jnp.float32)

    @pl.when(at.leads)
    def _():
        lead(at, raw, solved, inverted, lower, low_split, inverses, aug, upper)
        for k in range(n_leaf):
            factor[:, k * LEAF : (k + 1) * LEAF] = lower[k, pl.ds(pl.multiple_of(at.p * width, width), width), :]
        for b in range(n_leaf):
            inverted.sent(b)
        for b in range(n_leaf - 1):
            solved.sent(b)
        net.arrived()
        updated[...] = updated[...] - target[:, :width].T

    @pl.when(at.follows)
    def _():
        net.keep_own()

        full = slice(0, width)
        j_split = Split(j_high, j_low)

        def span(b, count=1):
            return slice(b * LEAF, (b + count) * LEAF)

        def store(dst, split, b, value):
            dst[:, span(b)] = value
            split.put(full, span(b), value)

        for b in range(n_leaf):
            if b == 0:
                for s in range(1, at.n_pos - 2):
                    for m in range(CHUNKS):
                        net.relay(s, m)
            if b in (2, 3):
                for m in ((0, 1), (2, 3))[b - 2]:
                    net.relay(at.n_pos - 2, m)
            if 3 <= b < 3 + CHUNKS:
                net.select(b - 3, window_rows, row_live)
            if b:
                solved.take(b - 1)
            if 3 <= b < 3 + CHUNKS:
                net.deal_all(b - 3)
            if 5 <= b < 5 + CHUNKS:
                net.dealt(b - 5)
            now = own[:, span(b)] * live
            if b:
                solved.taken(b - 1)
                low_split.put(slice(b * LEAF, total), span(b - 1), lower[b - 1, b * LEAF :, :])
                now = now - product(x_split.get(full, span(0, b)), low_split.get(span(b), span(0, b)))
            if b == n_leaf - 1:
                factor[:, span(b)] = now
                net.dealt(CHUNKS - 1)
                for k in range(0, n_leaf, 2):
                    left, right = target[:, span(k)], target[:, span(k + 1)]
                    if k:
                        both = product(j_split.get(full, span(0, k)), low_split.get(span(k, 2), span(0, k)))
                        left, right = left - both[:, :LEAF], right - both[:, LEAF:]
                    store(other, j_split, k, times_trans(left, inverses[k]))
                    right = right - product(j_split.get(full, span(k)), low_split.get(span(k + 1), span(k)))
                    if k + 1 < b:
                        store(other, j_split, k + 1, times_trans(right, inverses[k + 1]))
                    else:
                        other[:, span(b)] = right
                updated[...] = updated[...] - product(x_split.get(full, span(0, b)), j_split.get(full, span(0, b)))
                now = factor[:, span(b)]
            inverted.take(b)
            inverted.taken(b)
            now = times_trans(now, inverses[b])
            if b == n_leaf - 1:
                factor[:, span(b)] = now
                other[:, span(b)] = times_trans(other[:, span(b)], inverses[b])
            else:
                store(factor, x_split, b, now)
        solved.finish()
        inverted.finish()
        net.finish()


def factor_window(window_rows, row_live, panel, window, n_rows, n_cols):
    if n_cols != 4 or n_rows < 6 or n_rows % 2:
        raise ValueError("unsupported mesh")
    width, total = panel.shape
    n_leaf = total // LEAF
    n_raw = n_leaf + width // LEAF + 1
    n_low = n_leaf - 1
    n_pos = n_rows // 2
    chunk = width // n_cols // CHUNKS
    dma = pltpu.SemaphoreType.DMA
    tall = jax.ShapeDtypeStruct(panel.shape, jnp.float32)
    return pl.pallas_call(
        functools.partial(window_kernel, n_rows, n_cols),
        out_shape=(tall, tall, jax.ShapeDtypeStruct(window.shape, jnp.float32)),
        in_specs=[pl.BlockSpec(memory_space=pltpu.HBM)] * 4,
        out_specs=(pl.BlockSpec(memory_space=pltpu.VMEM),) * 3,
        scratch_shapes=[
            pltpu.SMEM(window_rows.shape, jnp.int32),
            pltpu.SMEM(row_live.shape, jnp.int32),
            pltpu.VMEM(panel.shape, jnp.float32),
            pltpu.VMEM((n_leaf, total, LEAF), jnp.float32),
            pltpu.VMEM(panel.shape, jnp.float32),
            pltpu.VMEM((n_leaf, LEAF, LEAF), jnp.float32),
            pltpu.VMEM((LEAF, 2 * LEAF), jnp.float32),
            pltpu.VMEM((LEAF, LEAF), jnp.float32),
            pltpu.VMEM((total, total), jnp.bfloat16),
            pltpu.VMEM((total, total), jnp.bfloat16),
            pltpu.VMEM(panel.shape, jnp.bfloat16),
            pltpu.VMEM(panel.shape, jnp.bfloat16),
            pltpu.VMEM(panel.shape, jnp.bfloat16),
            pltpu.VMEM(panel.shape, jnp.bfloat16),
        ] + [pltpu.VMEM((n_rows, chunk, total), jnp.float32)] * CHUNKS
        + [pltpu.VMEM((n_cols, chunk, total), jnp.float32)] * CHUNKS
        + [
            dma(()), dma(()), dma(()), dma(()), dma((n_leaf,)),
            dma((n_pos - 1,)),
            dma((n_raw,)), dma((n_raw,)), dma((n_raw,)), dma((n_raw,)),
            dma((n_low,)), dma((n_low,)), dma((n_low,)), dma((n_low,)),
            dma((n_leaf,)), dma((n_leaf,)), dma((n_leaf,)), dma((n_leaf,)),
            dma((n_pos, CHUNKS)), dma((n_pos, CHUNKS)), dma((n_pos, CHUNKS)), dma((n_pos, CHUNKS)),
            dma((n_pos, CHUNKS)), dma((n_pos, CHUNKS)),
            dma((n_cols, CHUNKS)), dma((n_cols, CHUNKS)), dma((n_cols, CHUNKS)), dma((n_cols, CHUNKS)),
        ],
        compiler_params=pltpu.CompilerParams(
            collective_id=0, has_side_effects=True, vmem_limit_bytes=(29 << 20) + n_rows * n_cols * CHUNKS * chunk * total),
        cost_estimate=pl.CostEstimate(flops=10**10, bytes_accessed=10**7, transcendentals=0),
        name="factor_window",
    )(*[pltpu.with_memory_space_constraint(x, pltpu.HBM) for x in (window_rows, row_live, panel, window)])


def update_kernel(factor, other, partial, factor_out, updated, sem):
    store = pltpu.make_async_copy(factor, factor_out, sem)
    store.start()
    r = lax.axis_index("rows")
    lo = factor.shape[1] - LEAF

    @pl.when(r < P_SIZE)
    def _():
        updated[...] = partial[...]

    @pl.when(r >= P_SIZE)
    def _():
        updated[...] = partial[...] - times_trans(factor[:, lo:], other[:, lo:])

    store.wait()


def update_window(factor, other, partial):
    return pl.pallas_call(
        update_kernel,
        out_shape=(jax.ShapeDtypeStruct(factor.shape, jnp.float32),
                   jax.ShapeDtypeStruct(partial.shape, jnp.float32)),
        in_specs=[pl.BlockSpec(memory_space=pltpu.VMEM)] * 3,
        out_specs=(pl.BlockSpec(memory_space=pltpu.HBM), pl.BlockSpec(memory_space=pltpu.VMEM)),
        scratch_shapes=[pltpu.SemaphoreType.DMA(())],
        compiler_params=pltpu.CompilerParams(vmem_limit_bytes=24 << 20),
        cost_estimate=pl.CostEstimate(flops=10**9, bytes_accessed=10**7, transcendentals=0),
        name="update_window",
    )(factor, other, partial)


def shards(n_rows, n_cols, panel, window_block, row_live, window_rows):
    factor, other, partial = factor_window(window_rows, row_live, panel, window_block, n_rows, n_cols)
    return update_window(factor, other, partial)


def solution(mesh):
    in_specs = (P("rows", None), P("rows", "cols"), P(), P())
    out_specs = (P("rows", None), P("rows", "cols"))
    body = functools.partial(shards, mesh.shape["rows"], mesh.shape["cols"])
    return jax.shard_map(body, mesh=mesh, in_specs=in_specs, out_specs=out_specs, check_vma=False)
```

time: 125 us -> 80.6 us (0.64)
  Pallas kernels: 123 us -> 78.9 us
    pallas_call x1, Pallas kernels: 121 us -> 76.6 us  [factor_window(): pl.pallas_call(functools.partial(window_kernel, n_rows, n_cols), out_shap...]
where the time goes in v4:
time: 80.6 us; the launch traced here: 79.7 us
  Pallas kernels  78.9 us (98%)
  between operations  0.82 us (1%)
    pallas_call x1, Pallas kernels, factor_window(): pl.pallas_call(functools.partial(window_kernel, n_rows, n_cols), out_shap...  76.6 us
    pallas_call x1, Pallas kernels, update_window(): pl.pallas_call(update_kernel, out_shape=(jax.ShapeDtypeStruct(factor.shap...  2.3 us

profile of v4, /device:TPU:27, one launch (start us, length us, event | category | flops | bytes accessed | tf_op | source)
XLA Modules:
  0.0 79.7 jit_solution(2987593609784616650)
XLA Ops:
  0.6 76.6 %factor_window.1 = (f32[512,1024]{1,0:T(8,128)S(1)}, f32[512,1024]{1,0:T(8,128)S(1)}, f32[512,512]{1,0:T(8,128)S(1)}) custom-call(s32[4]{0:T(128)} %rows_in.1, s32[8]{0:T(128)} %live_in.1, f32[512,1024]{1,0:T(8,128)} %panel.1, f32[512,512]{1,0:T(8,128)} %window.1), custom_call_target="tpu_custom_call" | custom-call | flops 10000000000 | bytes 10000000 | tf_op jit(solution)/shard_map/factor_window/pallas_call | solution.py:617
  77.3 2.3 %update_window.1 = (f32[512,1024]{1,0:T(8,128)}, f32[512,512]{1,0:T(8,128)}) custom-call(f32[512,1024]{1,0:T(8,128)S(1)} %get-tuple-element.5.factor, f32[512,1024]{1,0:T(8,128)S(1)} %get-tuple-element.6.other, f32[512,512]{1,0:T(8,128)S(1)} %get-tuple-element.7.partial), custom_call_target="tpu_custom_call" | custom-call | flops 1000000000 | bytes 10000000 | tf_op jit(solution)/shard_map/update_window/pallas_call | solution.py:674

commit v5 on v4

--- a/solution.py
+++ b/solution.py
@@ -11,7 +11,13 @@
 CONTRACT = (((1,), (1,)), ((), ()))
 LEAF = 128
 GROUP = 16
-CHUNKS = 4
+CHUNKS = 8
+EARLY = 5
+INV_STRAIGHT = 2
+LOW_STRAIGHT = 1
+LATE = {1: (0, 1), 2: (2, 3, 4), 3: (5, 6, 7)}
+SELECT = {2: (0, 1), 3: (2, 3), 4: (4, 5), 5: (6, 7)}
+DEALT = {4: (0, 1), 5: (2, 3), 6: (4, 5), 7: (6, 7)}
 MESH = pl.DeviceIdType.MESH
 
 
@@ -129,12 +135,19 @@
         def _():
             for s in range(1, self.n_pos):
                 greet(self.r + 2 * s, self.c)
-            pl.semaphore_wait(sem, self.n_cols + self.n_pos - 1)
+            for i in range(1, self.n_cols):
+                greet(self.r + 2, lax.rem(self.c + i, self.n_cols))
+            pl.semaphore_wait(sem, 2 * self.n_cols + self.n_pos - 2)
 
         @pl.when(self.follows)
         def _():
             greet(self.p, self.c)
 
+            @pl.when(self.q == 1)
+            def _():
+                for i in range(1, self.n_cols):
+                    greet(self.p, lax.rem(self.c + i, self.n_cols))
+
             @pl.when(self.q >= 2)
             def _():
                 greet(self.r - 2, self.c)
@@ -143,7 +156,8 @@
             def _():
                 greet(self.r + 2, self.c)
 
-            extra = (self.q >= 2).astype(jnp.int32) + self.passes.astype(jnp.int32)
+            first = (self.q == 1).astype(jnp.int32)
+            extra = first * (self.n_cols - 1) + (1 - first) + self.passes.astype(jnp.int32)
             pl.semaphore_wait(sem, self.n_cols + 1 + extra)
 
 
@@ -202,19 +216,20 @@
 
 
 class Solved(Blocks):
-    def __init__(self, at, lower, pieces, sems, straight=None):
+    def __init__(self, at, lower, pieces, sems, straight, n_straight):
         super().__init__(at, lower, pieces, sems)
         self.straight = straight
+        self.first_straight = len(pieces) - n_straight
 
     def is_last(self, piece):
-        return self.straight is not None and piece + 1 == len(self.pieces)
+        return piece >= self.first_straight
 
     def sends(self, piece):
         if not self.is_last(piece):
             return [self.to_row(piece, self.at.r + 2)]
         spot = self.place(piece)
         return [
-            remote(spot, spot, self.straight.at[s - 1], self.row_recv.at[piece], self.at.r + 2 * s, self.at.c)
+            remote(spot, spot, self.straight.at[piece - self.first_straight, s - 1], self.row_recv.at[piece], self.at.r + 2 * s, self.at.c)
             for s in reversed(range(1, self.at.n_pos))
         ]
 
@@ -303,8 +318,6 @@
             def _():
                 self.chain("up", 1, m).start()
 
-            self.across(at.q, m, True).start()
-
     def keep_own(self):
         for m in range(CHUNKS):
             start = pl.multiple_of(self.at.c * self.share + m * self.chunk, 8)
@@ -316,20 +329,32 @@
         @pl.when(at.q + s < at.n_pos)
         def _():
             self.awaited("dn", s, m).wait_recv()
+
+            @pl.when(at.q >= 2)
+            def _():
+                self.chain("dn", s + 1, m).start()
+
+        @pl.when(at.q - s >= 1)
+        def _():
+            self.awaited("up", s, m).wait_recv()
+
+            @pl.when(at.passes)
+            def _():
+                self.chain("up", s + 1, m).start()
+
+    def cross(self, s, m):
+        at = self.at
+        if s == 0:
+            self.across(at.q, m, True).start()
+            return
+
+        @pl.when(at.q + s < at.n_pos)
+        def _():
             self.across(at.q + s, m, False).start()
 
-            @pl.when(at.q >= 2)
-            def _():
-                self.chain("dn", s + 1, m).start()
-
         @pl.when(at.q - s >= 1)
         def _():
-            self.awaited("up", s, m).wait_recv()
             self.across(at.q - s, m, False).start()
-
-            @pl.when(at.passes)
-            def _():
-                self.chain("up", s + 1, m).start()
 
     def select(self, m, rows, live):
         at = self.at
@@ -356,13 +381,19 @@
             def _():
                 self.deal(t, m).start()
 
-    def to_leader(self, owner, m):
-        at = self.at
+            @pl.when(self.at.q == 1)
+            def _():
+                self.to_leader(t, m).start()
+
+    def to_leader(self, t, m):
+        at = self.at
+        cols = pl.ds(pl.multiple_of(at.p * self.width, LEAF), self.width)
+        return remote(self.staged[m].at[t, :, cols], self.left_part(m, at.c), self.l_send.at[t, m],
+                      self.l_recv.at[at.c, m], at.p, t)
+
+    def left_part(self, m, owner):
         start = pl.multiple_of(owner * self.share + m * self.chunk, 8)
-        rows = pl.ds(start, self.chunk)
-        src = self.target.at[rows, pl.ds(pl.multiple_of(at.p * self.width, LEAF), self.width)]
-        return remote(src, self.target.at[rows, pl.ds(0, self.width)], self.l_send.at[owner, m],
-                      self.l_recv.at[owner, m], at.p, at.c)
+        return self.target.at[pl.ds(start, self.chunk), pl.ds(0, self.width)]
 
     def dealt(self, m):
         at = self.at
@@ -371,15 +402,12 @@
             spot = self.part(self.target, m, src)
             remote(spot, spot, self.t_send.at[src, m], self.t_recv.at[src, m], at.r, src).wait_recv()
 
-        @pl.when(at.q == 1)
-        def _():
-            for owner in range(at.n_cols):
-                self.to_leader(owner, m).start()
-
     def arrived(self):
         for m in range(CHUNKS):
             for owner in range(self.at.n_cols):
-                self.to_leader(owner, m).wait_recv()
+                spot = self.left_part(m, owner)
+                remote(spot, spot, self.l_send.at[owner, m], self.l_recv.at[owner, m],
+                       self.at.r, self.at.c).wait_recv()
 
     def finish(self):
         at = self.at
@@ -475,12 +503,12 @@
         for k in range(n_leaf) for which in range(2) if k < (which + 1) * per and (k, which) != (0, 0)
     ]
     low_pieces = [(0, (k + 1) * LEAF, total - (k + 1) * LEAF, k) for k in range(n_leaf - 1)]
-    raw = Raw(at, lower, raw_pieces, sems[1:5])
-    solved = Solved(at, lower, low_pieces, sems[5:9])
+    raw = Raw(at, lower, raw_pieces, sems[2:6])
+    solved = Solved(at, lower, low_pieces, sems[6:10], sems[1], LOW_STRAIGHT)
     inv_pieces = [(0, 0, LEAF, k) for k in range(n_leaf)]
-    inverted = Solved(at, inverses, inv_pieces, sems[9:13], sems[0])
+    inverted = Solved(at, inverses, inv_pieces, sems[10:14], sems[0], INV_STRAIGHT)
     low_split, x_split = Split(low_high, low_low), Split(x_high, x_low)
-    net = Rows(at, panel, own, target, gathered, staged, sems[13:])
+    net = Rows(at, panel, own, target, gathered, staged, sems[14:])
     fetches = [
         pltpu.make_async_copy(window, updated, window_sem),
         pltpu.make_async_copy(rows_in, window_rows, rows_sem),
@@ -553,44 +581,88 @@
             dst[:, span(b)] = value
             split.put(full, span(b), value)
 
+        share = width // n_cols
+        halves_of = [[slice(c * share + h * share // 2, c * share + (h + 1) * share // 2) for c in range(n_cols)]
+                     for h in range(2)]
+
+        def gather(ref, h, cols):
+            return jnp.concatenate([ref[rows, cols] for rows in halves_of[h]], axis=0)
+
+        def scatter(ref, h, cols, value):
+            size = share // 2
+            for i, rows in enumerate(halves_of[h]):
+                ref[rows, cols] = value[i * size : (i + 1) * size]
+
+        def keep_j(h, b, value):
+            scatter(other, h, span(b), value)
+            for ref, part in zip((j_high, j_low), halves(value)):
+                scatter(ref, h, span(b), part)
+
+        def window_rows_step(h, k):
+            def j_get(cols):
+                return gather(j_high, h, cols), gather(j_low, h, cols)
+
+            left, right = gather(target, h, span(k)), gather(target, h, span(k + 1))
+            if k:
+                both = product(j_get(span(0, k)), low_split.get(span(k, 2), span(0, k)))
+                left, right = left - both[:, :LEAF], right - both[:, LEAF:]
+            left = times_trans(left, inverses[k])
+            keep_j(h, k, left)
+            right = right - product(halves(left), low_split.get(span(k + 1), span(k)))
+            if k + 2 < n_leaf:
+                keep_j(h, k + 1, times_trans(right, inverses[k + 1]))
+            else:
+                scatter(other, h, span(k + 1), right)
+
+        def cross(m):
+            for s in range(at.n_pos - 2):
+                net.cross(s, m)
+
         for b in range(n_leaf):
             if b == 0:
-                for s in range(1, at.n_pos - 2):
-                    for m in range(CHUNKS):
+                for m in range(CHUNKS):
+                    for s in range(1, at.n_pos - 2):
                         net.relay(s, m)
-            if b in (2, 3):
-                for m in ((0, 1), (2, 3))[b - 2]:
-                    net.relay(at.n_pos - 2, m)
-            if 3 <= b < 3 + CHUNKS:
-                net.select(b - 3, window_rows, row_live)
-            if b:
-                solved.take(b - 1)
-            if 3 <= b < 3 + CHUNKS:
-                net.deal_all(b - 3)
-            if 5 <= b < 5 + CHUNKS:
-                net.dealt(b - 5)
-            now = own[:, span(b)] * live
+                    if m < EARLY:
+                        cross(m)
+            if b == n_leaf - 2:
+                for k in range(0, n_leaf - 2, 2):
+                    window_rows_step(0, k)
+            for m in LATE.get(b, ()):
+                net.relay(at.n_pos - 2, m)
+                net.cross(at.n_pos - 2, m)
+            if b and EARLY + b - 1 < CHUNKS:
+                cross(EARLY + b - 1)
+            for m in SELECT.get(b, ()):
+                net.select(m, window_rows, row_live)
+            if b + 1 < n_leaf:
+                inverted.take(b)
+            for m in SELECT.get(b, ()):
+                net.deal_all(m)
             if b:
                 solved.taken(b - 1)
                 low_split.put(slice(b * LEAF, total), span(b - 1), lower[b - 1, b * LEAF :, :])
-                now = now - product(x_split.get(full, span(0, b)), low_split.get(span(b), span(0, b)))
+            if b % 2:
+                now = factor[:, span(b)] - product(
+                    x_split.get(full, span(b - 1)), low_split.get(span(b), span(b - 1)))
+            else:
+                pair = own[:, span(b, 2)] * live
+                if b:
+                    pair = pair - product(x_split.get(full, span(0, b)), low_split.get(span(b, 2), span(0, b)))
+                now = pair[:, :LEAF]
+                factor[:, span(b + 1)] = pair[:, LEAF:]
+            for m in DEALT.get(b, ()):
+                net.dealt(m)
             if b == n_leaf - 1:
                 factor[:, span(b)] = now
-                net.dealt(CHUNKS - 1)
-                for k in range(0, n_leaf, 2):
-                    left, right = target[:, span(k)], target[:, span(k + 1)]
-                    if k:
-                        both = product(j_split.get(full, span(0, k)), low_split.get(span(k, 2), span(0, k)))
-                        left, right = left - both[:, :LEAF], right - both[:, LEAF:]
-                    store(other, j_split, k, times_trans(left, inverses[k]))
-                    right = right - product(j_split.get(full, span(k)), low_split.get(span(k + 1), span(k)))
-                    if k + 1 < b:
-                        store(other, j_split, k + 1, times_trans(right, inverses[k + 1]))
-                    else:
-                        other[:, span(b)] = right
+                for k in range(0, n_leaf - 2, 2):
+                    window_rows_step(1, k)
+                window_rows_step(0, n_leaf - 2)
+                window_rows_step(1, n_leaf - 2)
                 updated[...] = updated[...] - product(x_split.get(full, span(0, b)), j_split.get(full, span(0, b)))
                 now = factor[:, span(b)]
-            inverted.take(b)
+            if b + 1 == n_leaf:
+                inverted.take(b)
             inverted.taken(b)
             now = times_trans(now, inverses[b])
             if b == n_leaf - 1:
@@ -598,6 +670,7 @@
                 other[:, span(b)] = times_trans(other[:, span(b)], inverses[b])
             else:
                 store(factor, x_split, b, now)
+                solved.take(b)
         solved.finish()
         inverted.finish()
         net.finish()
@@ -638,7 +711,7 @@
         + [pltpu.VMEM((n_cols, chunk, total), jnp.float32)] * CHUNKS
         + [
             dma(()), dma(()), dma(()), dma(()), dma((n_leaf,)),
-            dma((n_pos - 1,)),
+            dma((INV_STRAIGHT, n_pos - 1)), dma((LOW_STRAIGHT, n_pos - 1)),
             dma((n_raw,)), dma((n_raw,)), dma((n_raw,)), dma((n_raw,)),
             dma((n_low,)), dma((n_low,)), dma((n_low,)), dma((n_low,)),
             dma((n_leaf,)), dma((n_leaf,)), dma((n_leaf,)), dma((n_leaf,)),

time: 80.6 us -> 75.1 us (0.932)
  Pallas kernels: 78.9 us -> 73.9 us
    pallas_call x1, Pallas kernels: 76.6 us -> 71.6 us  [factor_window(): pl.pallas_call(functools.partial(window_kernel, n_rows, n_cols), out_shap...]
where the time goes in v5:
time: 75.1 us; the launch traced here: 74.7 us
  Pallas kernels  73.9 us (98%)
  between operations  0.82 us (1%)
    pallas_call x1, Pallas kernels, factor_window(): pl.pallas_call(functools.partial(window_kernel, n_rows, n_cols), out_shap...  71.6 us
    pallas_call x1, Pallas kernels, update_window(): pl.pallas_call(update_kernel, out_shape=(jax.ShapeDtypeStruct(factor.shap...  2.3 us

profile of v5, /device:TPU:27, one launch (start us, length us, event | category | flops | bytes accessed | tf_op | source)
XLA Modules:
  0.0 74.7 jit_solution(17057686093231011350)
XLA Ops:
  0.6 71.6 %factor_window.1 = (f32[512,1024]{1,0:T(8,128)S(1)}, f32[512,1024]{1,0:T(8,128)S(1)}, f32[512,512]{1,0:T(8,128)S(1)}) custom-call(s32[4]{0:T(128)} %rows_in.1, s32[8]{0:T(128)} %live_in.1, f32[512,1024]{1,0:T(8,128)} %panel.1, f32[512,512]{1,0:T(8,128)} %window.1), custom_call_target="tpu_custom_call" | custom-call | flops 10000000000 | bytes 10000000 | tf_op jit(solution)/shard_map/factor_window/pallas_call | solution.py:690
  72.2 2.3 %update_window.1 = (f32[512,1024]{1,0:T(8,128)}, f32[512,512]{1,0:T(8,128)}) custom-call(f32[512,1024]{1,0:T(8,128)S(1)} %get-tuple-element.5.factor, f32[512,1024]{1,0:T(8,128)S(1)} %get-tuple-element.6.other, f32[512,512]{1,0:T(8,128)S(1)} %get-tuple-element.7.partial), custom_call_target="tpu_custom_call" | custom-call | flops 1000000000 | bytes 10000000 | tf_op jit(solution)/shard_map/update_window/pallas_call | solution.py:747

commit v6 on v5

--- a/solution.py
+++ b/solution.py
@@ -12,10 +12,10 @@
 LEAF = 128
 GROUP = 16
 CHUNKS = 8
-EARLY = 5
+EARLY = 6
 INV_STRAIGHT = 2
 LOW_STRAIGHT = 1
-LATE = {1: (0, 1), 2: (2, 3, 4), 3: (5, 6, 7)}
+LATE = {1: (0, 1, 2), 2: (3, 4, 5), 3: (6, 7)}
 SELECT = {2: (0, 1), 3: (2, 3), 4: (4, 5), 5: (6, 7)}
 DEALT = {4: (0, 1), 5: (2, 3), 6: (4, 5), 7: (6, 7)}
 MESH = pl.DeviceIdType.MESH
@@ -448,13 +448,15 @@
     raw.come(first[0])
     raw.done(first[0])
 
+    def mirror(b):
+        block = lower[b, b * LEAF : (b + 1) * LEAF, :]
+        lower[b, b * LEAF : (b + 1) * LEAF, :] = jnp.where(rows >= lanes, block, block.T)
+
     def step(k, carry):
         here = pl.ds(pl.multiple_of(k * LEAF, LEAF), LEAF)
-        block = lower[k, here, :]
-        aug[:, :LEAF] = jnp.where(rows >= lanes, block, block.T)
+        aug[:, :LEAF] = lower[k, here, :]
         aug[:, LEAF:] = jnp.where(rows == lanes, 1.0, 0.0)
         factor_leaf(aug, upper, inverses.at[k])
-        lower[k, here, :] = upper[...].T
         for b in range(n_leaf):
 
             @pl.when(k == b)
@@ -478,12 +480,15 @@
                     lower[b, hi:, :] = column
                     split.put(slice(hi, total), slice(lo, hi), column)
                     nxt = hi + LEAF
+                    mirror(b + 1)
                     lower[b + 1, hi:, :] = lower[b + 1, hi:, :] - product(
                         split.get(slice(hi, total), slice(0, hi)), split.get(slice(hi, nxt), slice(0, hi)))
                     solved.send(b)
 
+        lower[k, here, :] = upper[...].T
         return carry
 
+    mirror(0)
     lax.fori_loop(0, n_leaf, step, 0)
 
 

time: 75.1 us -> 74.7 us (level)
  no operation moved by 1% of the time
where the time goes in v6:
time: 74.7 us; the launch traced here: 74.4 us
  Pallas kernels  73.6 us (99%)
  between operations  0.82 us (1%)
    pallas_call x1, Pallas kernels, factor_window(): pl.pallas_call(functools.partial(window_kernel, n_rows, n_cols), out_shap...  71.3 us
    pallas_call x1, Pallas kernels, update_window(): pl.pallas_call(update_kernel, out_shape=(jax.ShapeDtypeStruct(factor.shap...  2.3 us

profile of v6, /device:TPU:27, one launch (start us, length us, event | category | flops | bytes accessed | tf_op | source)
XLA Modules:
  0.0 74.4 jit_solution(17380376841982480755)
XLA Ops:
  0.6 71.3 %factor_window.1 = (f32[512,1024]{1,0:T(8,128)S(1)}, f32[512,1024]{1,0:T(8,128)S(1)}, f32[512,512]{1,0:T(8,128)S(1)}) custom-call(s32[4]{0:T(128)} %rows_in.1, s32[8]{0:T(128)} %live_in.1, f32[512,1024]{1,0:T(8,128)} %panel.1, f32[512,512]{1,0:T(8,128)} %window.1), custom_call_target="tpu_custom_call" | custom-call | flops 10000000000 | bytes 10000000 | tf_op jit(solution)/shard_map/factor_window/pallas_call | solution.py:695
  72.0 2.3 %update_window.1 = (f32[512,1024]{1,0:T(8,128)}, f32[512,512]{1,0:T(8,128)}) custom-call(f32[512,1024]{1,0:T(8,128)S(1)} %get-tuple-element.5.factor, f32[512,1024]{1,0:T(8,128)S(1)} %get-tuple-element.6.other, f32[512,512]{1,0:T(8,128)S(1)} %get-tuple-element.7.partial), custom_call_target="tpu_custom_call" | custom-call | flops 1000000000 | bytes 10000000 | tf_op jit(solution)/shard_map/update_window/pallas_call | solution.py:752
